TPU v7x, 128 devices: a whole 4x4x4 slice. The times are simulated.
128 devices in a mesh: dp: 32 (over z, y, x_lo), tensor: 4 (over x_hi, core).
Axes of the slice: x: 4 (x_hi: 2, x_lo: 2; x = x_hi * 2 + x_lo), y: 4, z: 4, core: 2. Of those that a mesh axis runs over, the one named last changes fastest.
Arguments:
- patches: bfloat16 [32768, 1280], P('dp'), may hold values from -27 to 27
- norm_gain: float32 [1280], replicated, may hold values from 0.1 to 1.9
- norm_bias: float32 [1280], replicated, may hold values from -3 to 3
- first_weight: bfloat16 [5120, 5120], P(None, 'tensor'), may hold values from -0.078125 to 0.078125
- first_bias: float32 [5120], P('tensor'), may hold values from -3 to 3
- second_weight: bfloat16 [5120, 8192], P('tensor', 'dp'), may hold values from -0.078125 to 0.078125
- second_bias: float32 [8192], P('tensor'), may hold values from -2 to 2
- text_embeds: bfloat16 [16384, 8192], P('dp', 'tensor'), may hold values from -36 to 36
- final_gain: float32 [8192], P('tensor'), may hold values from 0.1 to 1.9
- image_grids: int32 [32, 4, 2], replicated, may hold values from 2 to 8, as said below
- routing: int32 [32, 4], replicated, may hold values from 0 to 3, each once within a row
Outputs:
- embeddings: bfloat16 [16384, 8192], P('dp', 'tensor')
- normed: bfloat16 [16384, 8192], P('dp', 'tensor')
Inputs may be any that keep to these rules, and one draw needn't show every extreme that they name: `image_grids`: each image is a grid of 3 to 8 rows by 2 to 8 columns of merged tokens; in every draw some image is 8 by 8. `routing`: each row names every offset 0 to 3 once.
All inputs are finite; a program needn't handle non-finite values.
Results may differ from a plain program's by a relative error of at most 0.006.
Values may be sent and summed in bfloat16 or wider, within the bound.
A program may use at most 128 MiB of HBM per device.

v0:
```python
import jax
import jax.numpy as jnp
from jax import lax
from jax.sharding import PartitionSpec as P

D = 8192


def swapped(value, axis, bit):
    mask = 2**bit
    pairs = [(source, source ^ mask) for source in range(lax.axis_size(axis))]
    return lax.ppermute(value, axis, pairs)


def cut_along(value, dim, size):
    before, after = (value.shape[:dim], value.shape[dim + 1 :])
    return jnp.moveaxis(value.reshape(*before, size, -1, *after), dim, 0)


def sum_at_owner(value, axis, dim):
    tiles = cut_along(value, dim, lax.axis_size(axis))
    arrived = lax.all_to_all(tiles, axis, split_axis=0, concat_axis=0, tiled=True)
    return arrived.astype(jnp.float32).sum(axis=0)


def passed_along(block, axis, distance):
    devices = range(lax.axis_size(axis))
    route = [((i - distance) % len(devices), i) for i in devices]
    return lax.ppermute(block, axis, route)


def sent_to_all(value, axis):
    size = lax.axis_size(axis)
    return lax.all_to_all(
        jnp.broadcast_to(value[None], (size, *value.shape)), axis, 0, 0, tiled=True
    )


def taken_together(value, axis):
    everything = sent_to_all(value, axis)
    return jnp.sum(everything, axis=0)


def join_ordered(mine, other, lower, axis):
    first = jnp.concatenate([mine, other], axis=axis)
    second = jnp.concatenate([other, mine], axis=axis)
    return jnp.where(lower, first, second)


def per_device(
    patches,
    norm_gain,
    norm_bias,
    first_weight,
    first_bias,
    second_weight,
    second_bias,
    text_embeds,
    final_gain,
    image_grids,
    routing,
):
    patch_values = patches.astype(jnp.float32)
    centered = patch_values - jnp.mean(patch_values, axis=-1, keepdims=True)
    variance = jnp.mean(centered * centered, axis=-1, keepdims=True)
    normed_patches = centered * lax.rsqrt(variance + 1e-06) * norm_gain + norm_bias
    merged = normed_patches.reshape(-1, first_weight.shape[0]).astype(jnp.bfloat16)
    hidden = jax.nn.gelu(
        jnp.dot(merged, first_weight, preferred_element_type=jnp.float32) + first_bias,
        approximate=False,
    ).astype(jnp.bfloat16)
    own_index = lax.axis_index("dp")
    shard_count = lax.axis_size("dp")
    slot_rows = hidden.shape[0]
    column_width = second_weight.shape[1]
    group_rows = hidden
    for bit in range(2):
        lower = own_index >> bit & 1 == 0
        partner_rows = swapped(group_rows, "dp", bit)
        group_rows = join_ordered(group_rows, partner_rows, lower, 0)
    weight_cols = second_weight
    for bit in range(2, shard_count.bit_length() - 1):
        lower = own_index >> bit & 1 == 0
        partner_cols = swapped(weight_cols, "dp", bit)
        weight_cols = join_ordered(weight_cols, partner_cols, lower, 1)
    tile = jnp.dot(group_rows, weight_cols, preferred_element_type=jnp.float32).astype(jnp.bfloat16)
    tile_width = tile.shape[1]
    pieces = tile.reshape(1, 4, slot_rows, tile_width)
    for bit in range(2):
        own_bit = own_index >> bit & 1
        sources = pieces.shape[0]
        remaining = pieces.shape[1] // 2
        split = pieces.reshape(sources, remaining, 2, slot_rows, tile_width)
        keep = lax.dynamic_index_in_dim(split, own_bit, 2, keepdims=False)
        send = lax.dynamic_index_in_dim(split, 1 - own_bit, 2, keepdims=False)
        received = swapped(send, "dp", bit)
        stacked = join_ordered(keep[None], received[None], own_bit == 0, 0)
        pieces = stacked.reshape(2 * sources, remaining, slot_rows, tile_width)
    ordered = pieces.reshape(4, slot_rows, tile_width // column_width, column_width)
    ordered = jnp.transpose(ordered, (1, 2, 0, 3)).reshape(slot_rows, tile_width * 4)
    partial_terms = ordered.astype(jnp.float32)
    summed = sum_at_owner(partial_terms.astype(jnp.bfloat16), "tensor", 1)
    projected = (summed + second_bias).astype(jnp.bfloat16)
    block_total = image_grids.shape[1]
    cap_rows = projected.shape[0] // block_total
    feature_width = projected.shape[1]
    block_rows = projected.reshape(block_total, cap_rows, feature_width)
    counts_all = image_grids[:, :, 0] * image_grids[:, :, 1]
    slot_ids = jnp.arange(block_total, dtype=jnp.int32)
    own_routing = lax.dynamic_index_in_dim(routing, own_index, 0, keepdims=False)
    seq_rows = text_embeds.shape[0]
    image_rows = jnp.zeros((seq_rows, feature_width), jnp.bfloat16)
    filled_rows = jnp.zeros((), jnp.int32)
    zero_index = jnp.zeros((), jnp.int32)
    for stride in range(block_total):
        own_block = jnp.sum(jnp.where(own_routing == stride, slot_ids, 0))
        outgoing = lax.dynamic_index_in_dim(block_rows, own_block, 0, keepdims=False)
        if stride > 0:
            incoming = passed_along(outgoing, "dp", stride)
        else:
            incoming = outgoing
        source_shard = (own_index - stride) % shard_count
        source_routing = lax.dynamic_index_in_dim(routing, source_shard, 0, keepdims=False)
        source_block = jnp.sum(jnp.where(source_routing == stride, slot_ids, 0))
        source_counts = lax.dynamic_index_in_dim(counts_all, source_shard, 0, keepdims=False)
        image_count = lax.dynamic_index_in_dim(source_counts, source_block, 0, keepdims=False)
        image_rows = lax.dynamic_update_slice(image_rows, incoming, (filled_rows, zero_index))
        filled_rows = filled_rows + image_count
    position = jnp.arange(seq_rows, dtype=jnp.int32)[:, None]
    embeddings = jnp.where(position < filled_rows, image_rows, text_embeds)
    embed_values = embeddings.astype(jnp.float32)
    square_total = taken_together(jnp.sum(embed_values * embed_values, axis=-1), "tensor")
    scale_rows = lax.rsqrt(square_total / D + 1e-06)
    normed = (embed_values * scale_rows[:, None] * final_gain).astype(jnp.bfloat16)
    return (embeddings, normed)


def solution(mesh):
    placed = (
        P("dp", None),
        P(),
        P(),
        P(None, "tensor"),
        P("tensor"),
        P("tensor", "dp"),
        P("tensor"),
        P("dp", "tensor"),
        P("tensor"),
        P(),
        P(),
    )
    return jax.shard_map(
        per_device,
        mesh=mesh,
        in_specs=placed,
        out_specs=(P("dp", "tensor"), P("dp", "tensor")),
        check_vma=False,
    )
```

profile of v0, /device:TPU:1, one launch (start us, length us, event | category | flops | bytes accessed | tf_op | source)
XLA Modules:
  0.0 336.0 jit_solution(5987680164926691229)
XLA Ops:
  0.6 3.8 %collective-permute-start.2 = (bf16[1280,256]{1,0:T(8,128)(2,1)}, bf16[1280,256]{1,0:T(8,128)(2,1)S(1)}, u32[]{:S(2)}, u32[]{:S(2)}) collective-permute-start(bf16[1280,256]{1,0:T(8,128)(2,1)} %param.16), channel_id=1, source_target_pairs={{0,16},{4,20},{8,24},{12,28},{16,0},{20,4},{24,8},{28,12},{32,48},... | collective-permute-start | bytes 1966088 | tf_op jit(solution)/shard_map/ppermute | solution.py:12
  6.8 12.1 %collective-permute-done.2 = bf16[1280,256]{1,0:T(8,128)(2,1)S(1)} collective-permute-done((bf16[1280,256]{1,0:T(8,128)(2,1)}, bf16[1280,256]{1,0:T(8,128)(2,1)S(1)}, u32[]{:S(2)}, u32[]{:S(2)}) %collective-permute-start.2) | collective-permute-done | bytes 655392 | tf_op jit(solution)/shard_map/ppermute | solution.py:12
  23.8 2.9 convert_element_type.32
  26.7 23.1 %collective-permute-done.3 = bf16[1280,512]{1,0:T(8,128)(2,1)} collective-permute-done((bf16[1280,512]{1,0:T(8,128)(2,1)}, bf16[1280,512]{1,0:T(8,128)(2,1)}, u32[]{:S(2)}, u32[]{:S(2)}) %collective-permute-start.3) | collective-permute-done | bytes 1310752 | tf_op jit(solution)/shard_map/ppermute | solution.py:12
  49.7 3.4 %maximum_select_fusion.8 = bf16[1280,1024]{1,0:T(8,128)(2,1)S(1)} fusion(bf16[1280,512]{1,0:T(8,128)(2,1)} %collective-permute-done.3, bf16[1280,512]{1,0:T(8,128)(2,1)} %maximum_select_fusion.10, pred[]{:T(512)S(6)} %eq.81), kind=kLoop, calls=%fused_computation.32 | loop fusion | flops 11796480 | bytes 5242881 | tf_op jit(solution)/shard_map/jit(_where)/select_n | solution.py:47
  53.2 3.3 collective-permute-start.4
  56.5 10.9 %fusion.25 = bf16[256,1280]{1,0:T(8,128)(2,1)S(1)} fusion(bf16[256,5120]{1,0:T(8,128)(2,1)S(1)} %copy-done.1, bf16[5120,1280]{1,0:T(8,128)(2,1)} %param.14, f32[1280]{0:T(1024)S(1)} %copy-done.9), kind=kOutput, calls=%fused_computation.43 | convolution fusion | flops 3377070080 | bytes 16389120 | tf_op jit(solution)/shard_map/dot_general | solution.py:69
  68.7 12.5 %collective-permute-done = bf16[256,1280]{1,0:T(8,128)(2,1)} collective-permute-done((bf16[256,1280]{1,0:T(8,128)(2,1)S(1)}, bf16[256,1280]{1,0:T(8,128)(2,1)}, u32[]{:S(2)}, u32[]{:S(2)}) %collective-permute-start) | collective-permute-done | bytes 655392 | tf_op jit(solution)/shard_map/ppermute | solution.py:12
  81.2 2.7 maximum_select_fusion.9
  85.2 25.8 %collective-permute-done.1 = bf16[512,1280]{1,0:T(8,128)(2,1)} collective-permute-done((bf16[512,1280]{1,0:T(8,128)(2,1)}, bf16[512,1280]{1,0:T(8,128)(2,1)}, u32[]{:S(2)}, u32[]{:S(2)}) %collective-permute-start.1) | collective-permute-done | bytes 1310752 | tf_op jit(solution)/shard_map/ppermute | solution.py:12
  111.4 9.8 %fusion.16 = bf16[1024,2048]{1,0:T(8,128)(2,1)S(1)} fusion(bf16[1280,1024]{1,0:T(8,128)(2,1)} %collective-permute-done.4, bf16[1280,1024]{1,0:T(8,128)(2,1)S(1)} %maximum_select_fusion.8, pred[]{:T(512)S(6)} %eq.80, bf16[512,1280]{1,0:T(8,128)(2,1)} %collective-permute-done.1, bf16[512,1280]{1,0:T(8,128)(2,1)} %maximum_select_fusion.9, pred[]{:T(512)S(6)} %eq.78), kind=kOutput, calls=%fused_computation.24 | convolution fusion | flops 5406195712 | bytes 12058626 | tf_op jit(solution)/shard_map/dot_general | solution.py:86
  124.3 42.3 %collective-permute-done.5 = bf16[1,2,256,2048]{3,2,1,0:T(8,128)(2,1)} collective-permute-done((bf16[1,2,256,2048]{3,2,1,0:T(8,128)(2,1)}, bf16[1,2,256,2048]{3,2,1,0:T(8,128)(2,1)}, u32[]{:S(2)}, u32[]{:S(2)}) %collective-permute-start.5) | collective-permute-done | bytes 2097184 | tf_op jit(solution)/shard_map/ppermute | solution.py:12
  166.6 2.8 maximum_select_fusion.2
  171.4 41.1 %collective-permute-done.6 = bf16[2,1,256,2048]{3,2,0,1:T(8,128)(2,1)S(1)} collective-permute-done((bf16[2,1,256,2048]{3,2,0,1:T(8,128)(2,1)S(1)}, bf16[2,1,256,2048]{3,2,0,1:T(8,128)(2,1)S(1)}, u32[]{:S(2)}, u32[]{:S(2)}) %collective-permute-start.6) | collective-permute-done | bytes 2097184 | tf_op jit(solution)/shard_map/ppermute | solution.py:12
  214.7 6.2 %copy.41 = bf16[2,2,1,256,2048]{3,4,1,0,2:T(8,128)(2,1)} copy(bf16[2,2,1,256,2048]{4,3,1,2,0:T(8,128)(2,1)} %maximum_select_fusion.3) | data formatting | bytes 8388608 | tf_op jit(solution)/shard_map/jit(_where)/select_n | solution.py:47
  220.9 4.5 %copy.42 = bf16[256,8,4,256]{0,3,2,1:T(8,128)(2,1)} copy(bf16[256,8,4,256]{0,3,1,2:T(8,128)(2,1)} %bitcast.37) | data formatting | bytes 8388608 | tf_op jit(solution)/shard_map/transpose | solution.py:100
  225.5 10.6 %all-to-all-start = ((bf16[4,256,2048]{1,2,0:T(8,128)(2,1)}), bf16[4,256,2048]{1,2,0:T(8,128)(2,1)}, u32[]{:S(2)}, u32[]{:S(2)}) async-start(bf16[4,256,2048]{1,2,0:T(8,128)(2,1)} %bitcast.36), calls=%async_computation | async-start | bytes 8388608 | tf_op jit(solution)/shard_map/all_to_all | solution.py:22
  253.8 31.1 %all-to-all-done = bf16[4,256,2048]{1,2,0:T(8,128)(2,1)} async-done(((bf16[4,256,2048]{1,2,0:T(8,128)(2,1)}), bf16[4,256,2048]{1,2,0:T(8,128)(2,1)}, u32[]{:S(2)}, u32[]{:S(2)}) %all-to-all-start) | async-done | bytes 4194336 | tf_op jit(solution)/shard_map/all_to_all | solution.py:22
  284.9 3.0 convert_reduce_fusion
  301.4 3.1 collective-permute-done.7
  307.2 9.6 %collective-permute-done.8 = bf16[64,2048]{1,0:T(8,128)(2,1)} collective-permute-done((bf16[64,2048]{1,0:T(8,128)(2,1)S(1)}, bf16[64,2048]{1,0:T(8,128)(2,1)}, u32[]{:S(2)}, u32[]{:S(2)}) %collective-permute-start.8) | collective-permute-done | bytes 262176 | tf_op jit(solution)/shard_map/ppermute | solution.py:29
  321.2 3.7 %fusion.13 = (f32[512]{0:T(512)S(1)}, bf16[512,2048]{1,0:T(8,128)(2,1)}) fusion(bf16[512,2048]{1,0:T(8,128)(2,1)S(1)} %dynamic_update_slice.15, bf16[512,2048]{1,0:T(8,128)(2,1)} %param.18, pred[512]{0:T(512)(128)(4,1)S(1)} %iota_compare_fusion), kind=kLoop, calls=%fused_computation.19 | loop fusion | flops 4193792 | bytes 6294016 | tf_op jit(solution)/shard_map/reduce_sum | solution.py:132
  325.0 7.5 %all_to_all.11 = f32[4,1,512]{2,1,0:T(1,128)S(1)} all-to-all(f32[4,1,512]{2,1,0:T(1,128)S(1)} %broadcast_in_dim.20), channel_id=1, replica_groups=mesh['dp'=32,'tensor'=4] {'tensor'}, dimensions={0} | all-to-all | bytes 16384 | tf_op jit(solution)/shard_map/all_to_all | solution.py:34
  332.5 3.5 %fusion.15 = bf16[512,2048]{1,0:T(8,128)(2,1)} fusion(bf16[512,2048]{1,0:T(8,128)(2,1)} %get-tuple-element.11, f32[2048]{0:T(1024)S(1)} %copy-done.7, f32[512]{0:T(512)S(1)} %add_rsqrt_fusion.1), kind=kLoop, calls=%fused_computation.21 | loop fusion | flops 4194304 | bytes 4204544 | tf_op jit(solution)/shard_map/convert_element_type | solution.py:134
  (57 shorter events, 36.7 us)
Async XLA Ops:
  0.6 18.3 %copy-start.2 = (bf16[1280,256]{1,0:T(8,128)(2,1)S(1)}, bf16[1280,256]{1,0:T(8,128)(2,1)}, u32[]{:S(2)}) copy-start(bf16[1280,256]{1,0:T(8,128)(2,1)} %param.16) | copy-start | bytes 1966084
  0.6 18.2 %collective-permute-start.2 = (bf16[1280,256]{1,0:T(8,128)(2,1)}, bf16[1280,256]{1,0:T(8,128)(2,1)S(1)}, u32[]{:S(2)}, u32[]{:S(2)}) collective-permute-start(bf16[1280,256]{1,0:T(8,128)(2,1)} %param.16), channel_id=1, source_target_pairs={{0,16},{4,20},{8,24},{12,28},{16,0},{20,4},{24,8},{28,12},{32,48},... | collective-permute-start | bytes 1966088 | tf_op jit(solution)/shard_map/ppermute | solution.py:12
  4.5 17.4 %copy-start = (bf16[1024,1280]{1,0:T(8,128)(2,1)S(1)}, bf16[1024,1280]{1,0:T(8,128)(2,1)}, u32[]{:S(2)}) copy-start(bf16[1024,1280]{1,0:T(8,128)(2,1)} %param.11) | copy-start | bytes 7864324
  6.8 16.0 %copy-start.4 = (f32[1280]{0:T(1024)S(1)}, f32[1280]{0:T(1024)}, u32[]{:S(2)}) copy-start(f32[1280]{0:T(1024)} %param.13) | copy-start | bytes 15364
  6.8 16.0 %copy-start.5 = (f32[1280]{0:T(1024)S(1)}, f32[1280]{0:T(1024)}, u32[]{:S(2)}) copy-start(f32[1280]{0:T(1024)} %param.12) | copy-start | bytes 15364
  20.2 29.5 %collective-permute-start.3 = (bf16[1280,512]{1,0:T(8,128)(2,1)}, bf16[1280,512]{1,0:T(8,128)(2,1)}, u32[]{:S(2)}, u32[]{:S(2)}) collective-permute-start(bf16[1280,512]{1,0:T(8,128)(2,1)} %maximum_select_fusion.10), channel_id=1, source_target_pairs={{0,32},{4,36},{8,40},{12,44},{16,48},{20,52},{24,56},{28,60},{32,0... | collective-permute-start | bytes 3932168 | tf_op jit(solution)/shard_map/ppermute | solution.py:12
  26.7 29.8 %copy-start.1 = (bf16[256,5120]{1,0:T(8,128)(2,1)S(1)}, bf16[256,5120]{1,0:T(8,128)(2,1)}, u32[]{:S(2)}) copy-start(bf16[256,5120]{1,0:T(8,128)(2,1)} %convert_element_type.32) | copy-start | bytes 7864324
  26.7 29.8 %copy-start.9 = (f32[1280]{0:T(1024)S(1)}, f32[1280]{0:T(1024)}, u32[]{:S(2)}) copy-start(f32[1280]{0:T(1024)} %param.15) | copy-start | bytes 15364
  53.2 58.2 %collective-permute-start.4 = (bf16[1280,1024]{1,0:T(8,128)(2,1)S(1)}, bf16[1280,1024]{1,0:T(8,128)(2,1)}, u32[]{:S(2)}, u32[]{:S(2)}) collective-permute-start(bf16[1280,1024]{1,0:T(8,128)(2,1)S(1)} %maximum_select_fusion.8), channel_id=1, source_target_pairs={{0,64},{4,68},{8,72},{12,76},{16,80},{20,84},{24,88},{28,92},{32,9... | collective-permute-start | bytes 7864328 | tf_op jit(solution)/shard_map/ppermute | solution.py:12
  67.4 13.8 %collective-permute-start = (bf16[256,1280]{1,0:T(8,128)(2,1)S(1)}, bf16[256,1280]{1,0:T(8,128)(2,1)}, u32[]{:S(2)}, u32[]{:S(2)}) collective-permute-start(bf16[256,1280]{1,0:T(8,128)(2,1)S(1)} %fusion.25), channel_id=1, source_target_pairs={{0,4},{4,0},{8,12},{12,8},{16,20},{20,16},{24,28},{28,24},{32,36},... | collective-permute-start | bytes 1966088 | tf_op jit(solution)/shard_map/ppermute | solution.py:12
  83.9 27.1 %collective-permute-start.1 = (bf16[512,1280]{1,0:T(8,128)(2,1)}, bf16[512,1280]{1,0:T(8,128)(2,1)}, u32[]{:S(2)}, u32[]{:S(2)}) collective-permute-start(bf16[512,1280]{1,0:T(8,128)(2,1)} %maximum_select_fusion.9), channel_id=1, source_target_pairs={{0,8},{4,12},{8,0},{12,4},{16,24},{20,28},{24,16},{28,20},{32,40},... | collective-permute-start | bytes 3932168 | tf_op jit(solution)/shard_map/ppermute | solution.py:12
  123.0 43.5 %collective-permute-start.5 = (bf16[1,2,256,2048]{3,2,1,0:T(8,128)(2,1)}, bf16[1,2,256,2048]{3,2,1,0:T(8,128)(2,1)}, u32[]{:S(2)}, u32[]{:S(2)}) collective-permute-start(bf16[1,2,256,2048]{3,2,1,0:T(8,128)(2,1)} %get-tuple-element.15), channel_id=1, source_target_pairs={{0,4},{4,0},{8,12},{12,8},{16,20},{20,16},{24,28},{28,24},{32,36},... | collective-permute-start | bytes 6291464 | tf_op jit(solution)/shard_map/ppermute | solution.py:12
  170.0 42.4 %collective-permute-start.6 = (bf16[2,1,256,2048]{3,2,0,1:T(8,128)(2,1)S(1)}, bf16[2,1,256,2048]{3,2,0,1:T(8,128)(2,1)S(1)}, u32[]{:S(2)}, u32[]{:S(2)}) collective-permute-start(bf16[2,1,256,2048]{3,2,0,1:T(8,128)(2,1)S(1)} %get-tuple-element.13), channel_id=1, source_target_pairs={{0,8},{4,12},{8,0},{12,4},{16,24},{20,28},{24,16},{28,20},{32,40},... | collective-permute-start | bytes 6291464 | tf_op jit(solution)/shard_map/ppermute | solution.py:12
  225.5 10.6 %copy-start.3 = (s32[32,4]{0,1:T(4,128)S(1)}, s32[32,4]{0,1:T(4,128)}, u32[]{:S(2)}) copy-start(s32[32,4]{0,1:T(4,128)} %param.21) | copy-start | bytes 1540
  225.5 59.4 %all-to-all-start = ((bf16[4,256,2048]{1,2,0:T(8,128)(2,1)}), bf16[4,256,2048]{1,2,0:T(8,128)(2,1)}, u32[]{:S(2)}, u32[]{:S(2)}) async-start(bf16[4,256,2048]{1,2,0:T(8,128)(2,1)} %bitcast.36), calls=%async_computation | async-start | bytes 8388608 | tf_op jit(solution)/shard_map/all_to_all | solution.py:22
  287.9 1.8 copy-start.6
  289.7 6.5 %copy-start.8 = (s32[32,4,2]{0,2,1:T(2,128)S(1)}, s32[32,4,2]{0,2,1:T(2,128)}, u32[]{:S(2)}) copy-start(s32[32,4,2]{0,2,1:T(2,128)} %param.20) | copy-start | bytes 3076
  291.6 12.9 %collective-permute-start.7 = (bf16[64,2048]{1,0:T(8,128)(2,1)S(1)}, bf16[64,2048]{1,0:T(8,128)(2,1)}, u32[]{:S(2)}, u32[]{:S(2)}) collective-permute-start(bf16[64,2048]{1,0:T(8,128)(2,1)S(1)} %get-tuple-element.18), channel_id=1, source_target_pairs={{124,0},{0,4},{4,8},{8,12},{12,16},{16,20},{20,24},{24,28},{28,32}... | collective-permute-start | bytes 786440 | tf_op jit(solution)/shard_map/ppermute | solution.py:29
  292.9 23.8 %collective-permute-start.8 = (bf16[64,2048]{1,0:T(8,128)(2,1)S(1)}, bf16[64,2048]{1,0:T(8,128)(2,1)}, u32[]{:S(2)}, u32[]{:S(2)}) collective-permute-start(bf16[64,2048]{1,0:T(8,128)(2,1)S(1)} %get-tuple-element.17), channel_id=1, source_target_pairs={{120,0},{124,4},{0,8},{4,12},{8,16},{12,20},{16,24},{20,28},{24,32... | collective-permute-start | bytes 786440 | tf_op jit(solution)/shard_map/ppermute | solution.py:29
  294.2 25.3 %collective-permute-start.9 = (bf16[64,2048]{1,0:T(8,128)(2,1)S(1)}, bf16[64,2048]{1,0:T(8,128)(2,1)S(1)}, u32[]{:S(2)}, u32[]{:S(2)}) collective-permute-start(bf16[64,2048]{1,0:T(8,128)(2,1)S(1)} %get-tuple-element.16), channel_id=1, source_target_pairs={{116,0},{120,4},{124,8},{0,12},{4,16},{8,20},{12,24},{16,28},{20,3... | collective-permute-start | bytes 786440 | tf_op jit(solution)/shard_map/ppermute | solution.py:29
  321.2 11.3 %copy-start.7 = (f32[2048]{0:T(1024)S(1)}, f32[2048]{0:T(1024)}, u32[]{:S(2)}) copy-start(f32[2048]{0:T(1024)} %param.19) | copy-start | bytes 24580
where the time goes:
time: 337 us; the launch traced here: 336 us
  waiting for transfers between devices  201 us (60%)
  other arithmetic  31.7 us (9%)
  starting transfers between devices  29.1 us (9%)
  local copies, waits for them, and re-layouts  26 us (8%)
  matrix products  20.7 us (6%)
  between operations  19.9 us (6%)
  blocking collectives  7.51 us (2%)
    ppermute x7, waiting for transfers between devices, swapped(): return lax.ppermute(value, axis, pairs)  157 us
    all_to_all x1, waiting for transfers between devices, sum_at_owner(): lax.all_to_all(tiles, axis, split_axis=0, concat_axis=0, tiled=True)  31.1 us
    ppermute x7, starting transfers between devices, swapped(): return lax.ppermute(value, axis, pairs)  13.9 us
    ppermute x3, waiting for transfers between devices, passed_along(): return lax.ppermute(block, axis, route)  12.7 us
    select_n x5, other arithmetic, join_ordered(): return jnp.where(lower, first, second)  12.6 us
    dot_general x1, matrix products, per_device(): jnp.dot(merged, first_weight, preferred_element_type=jnp.float32)  10.9 us
    all_to_all x1, starting transfers between devices, sum_at_owner(): lax.all_to_all(tiles, axis, split_axis=0, concat_axis=0, tiled=True)  10.6 us
    dot_general x1, matrix products, per_device(): jnp.dot(group_rows, weight_cols, preferred_element_type=jnp.float32)  9.83 us
  transfers between devices with their start and end apart: 11, of which 10 were waited for; matrix products, arithmetic and copies ran while one was open for 9% of the time, Pallas kernels for 0%

commit v1 on v0

v1 whole, which is shorter than its diff:
```python
import functools

import jax
import jax.numpy as jnp
from jax import lax
from jax.experimental import pallas as pl
from jax.experimental.pallas import tpu as pltpu
from jax.sharding import PartitionSpec as P

MESH = pl.DeviceIdType.MESH
F32 = jnp.float32
BF16 = jnp.bfloat16
SHARDS = 32
CAP = 64
D = 8192
CH = 256
NCH = 5
HEAD = 192
SQRT_HALF = 0.7071067811865476


def wait_for(ref, sem):
    pltpu.make_async_copy(ref, ref, sem).wait()


def send(src, dst, send_sem, recv_sem, device):
    pltpu.make_async_remote_copy(
        src_ref=src,
        dst_ref=dst,
        send_sem=send_sem,
        recv_sem=recv_sem,
        device_id=device,
        device_id_type=MESH,
    ).start()


def row_squares(values):
    ones = jnp.ones((8, values.shape[1]), F32)
    return lax.dot_general(
        ones,
        values,
        (((1,), (1,)), ((), ())),
        precision=lax.Precision.HIGHEST,
        preferred_element_type=F32,
    )


def merge_kernel(
    routing_ref,
    pat_hbm,
    gain_ref,
    nbias_ref,
    w1_hbm,
    b1_ref,
    w2_hbm,
    b2_ref,
    text_hbm,
    img_out,
    sums_out,
    pat,
    w1,
    nbuf,
    mer,
    hid,
    wbuf,
    text,
    dsend,
    drecv,
    xsend,
    xrecv,
    fbuf,
    obuf,
    img,
    sbuf,
    lsem,
    s0,
    s_swap,
    s_w,
    s_h,
    s_d,
    s_x,
    s_i,
    s_s,
    r_om,
    r_op,
    r_p,
    r_fm,
    r_fp,
    r_pm,
    r_pp,
    r_p2,
    r_h1,
    r_h2,
    r_h3,
    r_d,
    r_x,
    r_i,
    r_s,
):
    d = lax.axis_index("dp")
    t = lax.axis_index("tensor")
    z = lax.div(d, 8)
    y = lax.rem(lax.div(d, 2), 4)
    xl = lax.rem(d, 2)
    xh = lax.div(t, 2)
    c = lax.rem(t, 2)
    zp = lax.rem(z + 1, 4)
    zm = lax.rem(z + 3, 4)
    zo = lax.rem(z + 2, 4)
    yb = y + 1 - 2 * lax.rem(y, 2)
    q = xl + xh - 2 * xl * xh
    dev_zp = (zp * 8 + y * 2 + xl, t)
    dev_zm = (zm * 8 + y * 2 + xl, t)
    dev_ya = (z * 8 + (3 - y) * 2 + xl, t)
    dev_yb = (z * 8 + yb * 2 + xl, t)
    dev_x = (z * 8 + y * 2 + 1 - xl, t)
    dev_cut = (z * 8 + y * 2 + 1 - xl, (1 - xh) * 2 + c)
    dev_core = (d, xh * 2 + 1 - c)

    pltpu.make_async_copy(pat_hbm, pat, lsem.at[NCH]).start()

    def w1_copy(n):
        return pltpu.make_async_copy(
            w1_hbm.at[:, pl.ds(n * CH, CH)], w1.at[n], lsem.at[n]
        )

    w1_copy(0).start()

    @pl.when(xh == 0)
    def _():
        for kc in range(NCH):
            pltpu.make_async_copy(
                w2_hbm.at[pl.ds(kc * CH, CH)], wbuf.at[z * 2, kc], s0.at[kc]
            ).start()

    for n in range(1, NCH):
        w1_copy(n).start()
    pltpu.make_async_copy(text_hbm, text, lsem.at[NCH + 1]).start()

    barrier = pltpu.get_barrier_semaphore()
    base = d - lax.rem(d, 4)

    def greet(device):
        pl.semaphore_signal(barrier, inc=1, device_id=device, device_id_type=MESH)

    for o in range(-4, 8):
        other = lax.rem(base + o + SHARDS, SHARDS)

        @pl.when(other != d)
        def _():
            greet((other, t))

    greet(dev_zp)
    greet(dev_zm)
    greet(dev_cut)
    for i in range(1, 4):
        greet((d, lax.rem(t + i, 4)))
    pl.semaphore_wait(barrier, 17)

    def own_send(kc):
        block = wbuf.at[z * 2, kc]
        wait_for(block, s0.at[kc])
        send(block, block, s_w, r_om.at[kc], dev_zp)
        send(block, block, s_w, r_op.at[kc], dev_zm)
        send(block, wbuf.at[z * 2 + 1, kc], s_w, r_p.at[kc], dev_ya)

    @pl.when(xh == 1)
    def _():
        for kc in range(NCH):
            send(
                w2_hbm.at[pl.ds(kc * CH, CH)],
                wbuf.at[z * 2, kc],
                s_swap,
                s0.at[kc],
                dev_x,
            )

    @pl.when(xh == 0)
    def _():
        for kc in range(NCH):
            own_send(kc)

    wait_for(pat, lsem.at[NCH])
    gain = gain_ref[...]
    nbias = nbias_ref[...]
    width = pat.shape[1]

    def norm_step(step, carry):
        slot = lax.div(step, 4)
        part = lax.rem(step, 4)
        values = jnp.zeros((64, width), F32)
        for b in range(4):
            start = pl.multiple_of(b * (4 * CAP) + part * 64, 64)
            chosen = (routing_ref[d, b] == slot).astype(F32)
            values = values + pat[pl.ds(start, 64), :].astype(F32) * chosen
        centered = values - jnp.mean(values, axis=-1, keepdims=True)
        variance = jnp.mean(centered * centered, axis=-1, keepdims=True)
        normed = centered * lax.rsqrt(variance + 1e-06) * gain + nbias
        row = pl.multiple_of(step * 16, 16)
        for i in range(width // 128):
            nbuf[i] = normed[:, i * 128 : (i + 1) * 128]
        for j in range(4):
            for i in range(width // 128):
                mer[pl.ds(row, 16), j * width + i * 128 : j * width + (i + 1) * 128] = (
                    nbuf[i, pl.ds(j, 16, stride=4), :].astype(BF16)
                )
        return carry

    lax.fori_loop(0, 16, norm_step, 0)

    def hidden_step(n, carry):
        wait_for(w1.at[n], lsem.at[n])
        value = jnp.dot(mer[...], w1[n], preferred_element_type=F32)
        value = value + b1_ref[pl.ds(n, 1), :]
        value = 0.5 * value * (1.0 + lax.erf(value * SQRT_HALF))
        hid[0, n] = value.astype(BF16)
        send(hid.at[0, n], hid.at[1, n], s_h, r_h1.at[n], dev_x)
        send(hid.at[0, n], hid.at[2, n], s_h, r_h2.at[n], dev_yb)

        @pl.when((xh == 1) & (lax.rem(n, 2) == 0))
        def _():
            own_send(lax.div(n, 2))

        return carry

    lax.fori_loop(0, NCH, hidden_step, 0)

    def relay_far(kc, carry):
        @pl.when((xh == 1) & (kc < 2))
        def _():
            own_send(kc + 3)

        wait_for(wbuf.at[zm * 2, kc], r_om.at[kc])
        upper = wbuf.at[zm * 2, kc, pl.ds(0, CH // 2)]
        send(upper, upper, s_w, r_fm.at[kc], dev_zp)
        wait_for(wbuf.at[zp * 2, kc], r_op.at[kc])
        under = wbuf.at[zp * 2, kc, pl.ds(CH // 2, CH // 2)]
        send(under, under, s_w, r_fp.at[kc], dev_zm)
        return carry

    lax.fori_loop(0, NCH, relay_far, 0)

    def relay_pair(kc, carry):
        block = wbuf.at[z * 2 + 1, kc]
        wait_for(block, r_p.at[kc])
        send(block, block, s_w, r_pm, dev_zp)
        send(block, block, s_w, r_pp, dev_zm)
        return carry

    lax.fori_loop(0, NCH, relay_pair, 0)

    wait_for(text, lsem.at[NCH + 1])

    def text_step(i, carry):
        rows = pl.ds(pl.multiple_of(i * CH, CH), CH)
        total = jnp.zeros((CH, CH), F32)
        for j in range(8):
            values = text[rows, j * CH : (j + 1) * CH].astype(F32)
            total = total + values * values
        sbuf[t, :, rows] = row_squares(total)
        return carry

    lax.fori_loop(0, 2, text_step, 0)

    def relay_rows(n, carry):
        wait_for(hid.at[1, n], r_h1.at[n])
        send(
            hid.at[1, n, pl.ds(0, HEAD)],
            hid.at[3, n, pl.ds(0, HEAD)],
            s_h,
            r_h3,
            dev_yb,
        )
        wait_for(hid.at[2, n], r_h2.at[n])
        send(
            hid.at[2, n, pl.ds(HEAD, CH - HEAD)],
            hid.at[3, n, pl.ds(HEAD, CH - HEAD)],
            s_h,
            r_h3,
            dev_x,
        )
        wait_for(wbuf.at[zo * 2, n, pl.ds(0, CH // 2)], r_fm.at[n])
        wait_for(wbuf.at[zo * 2, n, pl.ds(CH // 2, CH // 2)], r_fp.at[n])
        send(wbuf.at[zo * 2, n], wbuf.at[zo * 2 + 1, n], s_w, r_p2, dev_ya)
        return carry

    lax.fori_loop(0, NCH, relay_rows, 0)
    wait_for(hid.at[3], r_h3)

    def tile(r, group, p):
        total = jnp.dot(hid[r, 0], wbuf[group * 2 + p, 0], preferred_element_type=F32)
        for n in range(1, NCH):
            total = total + jnp.dot(
                hid[r, n], wbuf[group * 2 + p, n], preferred_element_type=F32
            )
        return total

    other = (1 - xh) * 2
    mine = xh * 2

    def to_core(half, p, group):
        def step(r, carry):
            dsend[half, p, r] = tile(r, group, p).astype(BF16)
            send(
                dsend.at[half, p, r],
                drecv.at[half, p, r],
                s_d,
                r_d.at[half * 8 + p * 4 + r],
                dev_core,
            )
            return carry

        lax.fori_loop(0, 4, step, 0)

    def across(p):
        def step(r, carry):
            value = tile(r, other + c, p)
            wait_for(drecv.at[0, p, r], r_d.at[p * 4 + r])
            value = value + drecv[0, p, r].astype(F32)
            xsend[p, r] = value.astype(BF16)
            there = r + 1 - 2 * lax.rem(r, 2)
            send(
                xsend.at[p, r], xrecv.at[p, there], s_x, r_x.at[p * 4 + there], dev_cut
            )
            return carry

        lax.fori_loop(0, 4, step, 0)

    def keep(p):
        column = pl.multiple_of((y + p * (3 - 2 * y)) * 512 + q * CH, CH)
        bias = b2_ref[:, pl.ds(column, CH)]

        def step(r, carry):
            value = tile(r, mine + c, p)
            wait_for(drecv.at[1, p, r], r_d.at[8 + p * 4 + r])
            fbuf[p, r] = value + drecv[1, p, r].astype(F32) + bias
            return carry

        lax.fori_loop(0, 4, step, 0)

    to_core(0, 0, other + 1 - c)
    across(0)
    wait_for(wbuf.at[zm * 2 + 1], r_pm)
    wait_for(wbuf.at[zp * 2 + 1], r_pp)
    wait_for(wbuf.at[zo * 2 + 1], r_p2)
    to_core(0, 1, other + 1 - c)
    across(1)
    to_core(1, 0, mine + 1 - c)
    to_core(1, 1, mine + 1 - c)
    keep(0)
    keep(1)

    def target(r, k):
        row_y = y + lax.div(r, 2) * (yb - y)
        row_x = xl + lax.rem(r, 2) * (1 - 2 * xl)
        return lax.rem(z * 8 + row_y * 2 + row_x + k, SHARDS)

    def pieces(p, r, k):
        rows = pl.ds(k * CAP, CAP)
        column = (y + p * (3 - 2 * y)) * 2 + q
        return obuf.at[p, r, rows], img.at[column, rows]

    for p in range(2):

        def finish(r, carry):
            wait_for(xrecv.at[p, r], r_x.at[p * 4 + r])
            obuf[p, r] = (fbuf[p, r] + xrecv[p, r].astype(F32)).astype(BF16)
            for k in range(4):
                e = target(r, k)
                src, dst = pieces(p, r, k)

                @pl.when(e == d)
                def _():
                    pltpu.make_async_copy(src, dst, r_i).start()

                @pl.when(e != d)
                def _():
                    send(src, dst, s_i.at[p * 16 + r * 4 + k], r_i, (e, t))

            return carry

        lax.fori_loop(0, 4, finish, 0)

    wait_for(img, r_i)
    img_copy = pltpu.make_async_copy(img, img_out, lsem.at[0])
    img_copy.start()
    total = jnp.zeros((CH, CH), F32)
    for b in range(8):
        values = img[b].astype(F32)
        total = total + values * values
    sbuf[t, :, pl.ds(512, CH)] = row_squares(total)
    for i in range(1, 4):
        send(
            sbuf.at[t],
            sbuf.at[t],
            s_s.at[i - 1],
            r_s.at[i - 1],
            (d, lax.rem(t + i, 4)),
        )
    for i in range(1, 4):
        wait_for(sbuf.at[lax.rem(t + 4 - i, 4)], r_s.at[i - 1])
    sums_copy = pltpu.make_async_copy(sbuf, sums_out, lsem.at[1])
    sums_copy.start()

    wait_for(wbuf.at[pl.ds(0, 7)], s_w)

    @pl.when(xh == 1)
    def _():
        wait_for(wbuf.at[0], s_swap)

    wait_for(hid.at[pl.ds(0, 3)], s_h)
    wait_for(dsend, s_d)
    wait_for(xsend, s_x)
    for p in range(2):

        def drain(r, carry):
            for k in range(4):
                src, _unused = pieces(p, r, k)

                @pl.when(target(r, k) != d)
                def _():
                    wait_for(src, s_i.at[p * 16 + r * 4 + k])

            return carry

        lax.fori_loop(0, 4, drain, 0)
    for i in range(1, 4):
        wait_for(sbuf.at[t], s_s.at[i - 1])
    img_copy.wait()
    sums_copy.wait()


def splice_kernel(
    grids_ref, routing_ref, text_ref, img_ref, sums_ref, gain_ref, emb_ref, out_ref
):
    d = lax.axis_index("dp")
    g = pl.program_id(0)
    rows = text_ref.shape[0]
    starts = []
    total = jnp.int32(0)
    for k in range(4):
        s = lax.rem(d + SHARDS - k, SHARDS)
        count = jnp.int32(0)
        for b in range(4):
            size = grids_ref[s, 2 * b] * grids_ref[s, 2 * b + 1]
            count = count + jnp.where(routing_ref[s, b] == k, size, 0)
        starts.append(total)
        total = total + count
    position = g * rows + lax.broadcasted_iota(jnp.int32, (rows, 1), 0)
    source = position
    for k in range(1, 4):
        begin = jnp.where(position >= starts[k], k * CAP - starts[k], 0)
        if k > 1:
            begin = begin - jnp.where(
                position >= starts[k], (k - 1) * CAP - starts[k - 1], 0
            )
        source = source + begin
    live = position < total
    sums = sums_ref[0] + sums_ref[1] + sums_ref[2] + sums_ref[3]
    sums = sums[0:1, :]
    index = jnp.where(live, 512 + source, position)
    lanes = lax.broadcasted_iota(jnp.int32, (rows, sums.shape[1]), 1)
    square = jnp.sum(jnp.where(lanes == index, sums, 0.0), axis=-1, keepdims=True)
    scale = lax.rsqrt(square / D + 1e-06)
    picks = jnp.where(
        lax.broadcasted_iota(jnp.int32, (rows, 4 * CAP), 1) == source, 1.0, 0.0
    ).astype(BF16)
    blocks = img_ref.shape[0]

    @pl.when(g * rows < 4 * CAP)
    def _():
        for b in range(blocks):
            cols = slice(b * CH, (b + 1) * CH)
            taken = jnp.dot(picks, img_ref[b], preferred_element_type=F32)
            value = jnp.where(live, taken, text_ref[:, cols].astype(F32))
            emb_ref[:, cols] = value.astype(BF16)
            out_ref[:, cols] = (value * scale * gain_ref[:, cols]).astype(BF16)

    @pl.when(g * rows >= 4 * CAP)
    def _():
        for b in range(blocks):
            cols = slice(b * CH, (b + 1) * CH)
            value = text_ref[:, cols].astype(F32)
            emb_ref[:, cols] = text_ref[:, cols]
            out_ref[:, cols] = (value * scale * gain_ref[:, cols]).astype(BF16)


def per_device(
    patches,
    norm_gain,
    norm_bias,
    first_weight,
    first_bias,
    second_weight,
    second_bias,
    text_embeds,
    final_gain,
    image_grids,
    routing,
):
    seq, features = text_embeds.shape
    width = patches.shape[1]
    hbm = pl.BlockSpec(memory_space=pl.ANY)
    vmem = pl.BlockSpec(memory_space=pltpu.VMEM)
    smem = pl.BlockSpec(memory_space=pltpu.SMEM)
    dma = pltpu.SemaphoreType.DMA
    img, sums = pl.pallas_call(
        merge_kernel,
        out_shape=(
            jax.ShapeDtypeStruct((8, CH, CH), BF16),
            jax.ShapeDtypeStruct((4, 8, seq + CH), F32),
        ),
        in_specs=[smem, hbm, vmem, vmem, hbm, vmem, hbm, vmem, hbm],
        out_specs=(hbm, hbm),
        scratch_shapes=[
            pltpu.VMEM(patches.shape, BF16),
            pltpu.VMEM((NCH, first_weight.shape[0], CH), BF16),
            pltpu.VMEM((width // 128, 64, 128), F32),
            pltpu.VMEM((CH, 4 * width), BF16),
            pltpu.VMEM((4, NCH, CH, CH), BF16),
            pltpu.VMEM((8, NCH, CH, CH), BF16),
            pltpu.VMEM((seq, features), BF16),
            pltpu.VMEM((2, 2, 4, CH, CH), BF16),
            pltpu.VMEM((2, 2, 4, CH, CH), BF16),
            pltpu.VMEM((2, 4, CH, CH), BF16),
            pltpu.VMEM((2, 4, CH, CH), BF16),
            pltpu.VMEM((2, 4, CH, CH), F32),
            pltpu.VMEM((2, 4, CH, CH), BF16),
            pltpu.VMEM((8, CH, CH), BF16),
            pltpu.VMEM((4, 8, seq + CH), F32),
            dma((NCH + 2,)),
            dma((NCH,)),
            dma,
            dma,
            dma,
            dma,
            dma,
            dma((32,)),
            dma((3,)),
            dma((NCH,)),
            dma((NCH,)),
            dma((NCH,)),
            dma((NCH,)),
            dma((NCH,)),
            dma,
            dma,
            dma,
            dma((NCH,)),
            dma((NCH,)),
            dma,
            dma((16,)),
            dma((8,)),
            dma,
            dma((3,)),
        ],
        compiler_params=pltpu.CompilerParams(
            collective_id=0, has_side_effects=True, vmem_limit_bytes=60 * 1024 * 1024
        ),
        name="merge",
    )(
        routing,
        patches,
        norm_gain.reshape(1, -1),
        norm_bias.reshape(1, -1),
        first_weight,
        first_bias.reshape(NCH, CH),
        second_weight,
        second_bias.reshape(1, -1),
        text_embeds,
    )
    rows = 128
    return pl.pallas_call(
        splice_kernel,
        grid=(seq // rows,),
        out_shape=(
            jax.ShapeDtypeStruct((seq, features), BF16),
            jax.ShapeDtypeStruct((seq, features), BF16),
        ),
        in_specs=[
            smem,
            smem,
            pl.BlockSpec((rows, features), lambda g: (g, 0)),
            vmem,
            vmem,
            vmem,
        ],
        out_specs=(
            pl.BlockSpec((rows, features), lambda g: (g, 0)),
            pl.BlockSpec((rows, features), lambda g: (g, 0)),
        ),
        name="splice",
    )(
        image_grids.reshape(SHARDS, -1),
        routing,
        text_embeds,
        img,
        sums,
        final_gain.reshape(1, -1),
    )


def solution(mesh):
    placed = (
        P("dp", None),
        P(),
        P(),
        P(None, "tensor"),
        P("tensor"),
        P("tensor", "dp"),
        P("tensor"),
        P("dp", "tensor"),
        P("tensor"),
        P(),
        P(),
    )
    return jax.shard_map(
        per_device,
        mesh=mesh,
        in_specs=placed,
        out_specs=(P("dp", "tensor"), P("dp", "tensor")),
        check_vma=False,
    )
```

time: 337 us -> 101 us (0.30)
  waiting for transfers between devices: 201 us -> 0 us
  Pallas kernels: 0 us -> 93 us
  other arithmetic: 31.7 us -> 0 us
  starting transfers between devices: 29.1 us -> 0 us
  matrix products: 20.7 us -> 0 us
  local copies, waits for them, and re-layouts: 26 us -> 6.6 us
  between operations: 19.9 us -> 0.64 us
  blocking collectives: 7.51 us -> 0 us
    ppermute x10 -> x0, waiting for transfers between devices: 170 us -> none  [the longest x7 157 us: swapped(): return lax.ppermute(value, axis, pairs)]
    pallas_call x0 -> x2, Pallas kernels: none -> 93 us  [the longest x1 87.5 us: per_device(): pl.pallas_call(merge_kernel, out_shape=(jax.ShapeDtypeStruct((8, CH, CH),...]
    all_to_all x1 -> x0, waiting for transfers between devices: 31.1 us -> none  [sum_at_owner(): lax.all_to_all(tiles, axis, split_axis=0, concat_axis=0, tiled=True)]
    dot_general x2 -> x0, matrix products: 20.7 us -> none  [the longest x1 10.9 us: per_device(): jnp.dot(merged, first_weight, preferred_element_type=jnp.float32)]
    ppermute x10 -> x0, starting transfers between devices: 18.4 us -> none  [the longest x7 13.9 us: swapped(): return lax.ppermute(value, axis, pairs)]
    select_n x5 -> x0, other arithmetic: 12.6 us -> none  [join_ordered(): return jnp.where(lower, first, second)]
    reduce_sum x9 -> x0, other arithmetic: 12.5 us -> none  [the longest x1 3.73 us: per_device(): jnp.sum(embed_values * embed_values, axis=-1)]
    all_to_all x1 -> x0, starting transfers between devices: 10.6 us -> none  [sum_at_owner(): lax.all_to_all(tiles, axis, split_axis=0, concat_axis=0, tiled=True)]
  transfers between devices with their start and end apart: 11 -> 0, of which waited for: 10 -> 0; matrix products, arithmetic and copies ran while one was open for 9% -> 0% of each run, Pallas kernels for 0% -> 0%
where the time goes in v1:
time: 101 us; the launch traced here: 100 us
  Pallas kernels  93 us (92%)
  local copies, waits for them, and re-layouts  6.6 us (7%)
    pallas_call x1, Pallas kernels, per_device(): pl.pallas_call(merge_kernel, out_shape=(jax.ShapeDtypeStruct((8, CH, CH),...  87.5 us
    pallas_call x1, Pallas kernels, per_device(): pl.pallas_call(splice_kernel, grid=(seq // rows,), out_shape=(jax.ShapeDt...  5.46 us

profile of v1, /device:TPU:1, one launch (start us, length us, event | category | flops | bytes accessed | tf_op | source)
XLA Modules:
  0.0 100.2 jit_solution(6895061792306950074)
XLA Ops:
  0.6 1.3 %reshape.23.gain_ref = f32[1,1280]{1,0:T(1,128)} reshape(f32[1280]{0:T(1024)} %param.12) | data formatting | bytes 10240 | tf_op jit(solution)/shard_map/reshape | solution.py:563
  1.9 1.3 %reshape.24.nbias_ref = f32[1,1280]{1,0:T(1,128)} reshape(f32[1280]{0:T(1024)} %param.13) | data formatting | bytes 10240 | tf_op jit(solution)/shard_map/reshape | solution.py:564
  3.2 1.3 %reshape.25.b1_ref = f32[5,256]{1,0:T(8,128)} reshape(f32[1280]{0:T(1024)} %param.15) | data formatting | bytes 10240 | tf_op jit(solution)/shard_map/reshape | solution.py:566
  4.5 1.4 %copy.18.routing_ref = s32[32,4]{1,0:T(8,128)} copy(s32[32,4]{0,1:T(4,128)} %param.21) | data formatting | bytes 1024 | tf_op args[10]
  5.9 1.4 %copy.17.grids_ref = s32[32,8]{1,0:T(8,128)} copy(s32[32,8]{0,1:T(8,128)} %bitcast.5) | data formatting | bytes 2048 | tf_op jit(solution)/shard_map/reshape | solution.py:593
  7.2 87.5 %merge.1 = (bf16[8,256,256]{2,1,0:T(8,128)(2,1)}, f32[4,8,768]{2,1,0:T(8,128)}) custom-call(s32[32,4]{1,0:T(8,128)} %copy.18.routing_ref, bf16[1024,1280]{1,0:T(8,128)(2,1)} %pat_hbm.1, f32[1,1280]{1,0:T(1,128)} %reshape.23.gain_ref, f32[1,1280]{1,0:T(1,128)} %reshape.24.nbias_ref, bf16[5120,1280]{1,0:T(8,128)(2,1)} %w1_hbm.1, f32[5,256]{1,0:T(8,128)} %reshape.25.b1_ref, ...), custom_call_target="tpu_custom_call" | custom-call | tf_op jit(solution)/shard_map/merge/pallas_call | solution.py:507
  94.7 5.5 %splice.1 = (bf16[512,2048]{1,0:T(8,128)(2,1)}, bf16[512,2048]{1,0:T(8,128)(2,1)}) custom-call(s32[32,8]{1,0:T(8,128)} %copy.17.grids_ref, s32[32,4]{1,0:T(8,128)} %copy.18.routing_ref, bf16[512,2048]{1,0:T(8,128)(2,1)} %text_ref.1, bf16[8,256,256]{2,1,0:T(8,128)(2,1)} %get-tuple-element.4.img_ref, f32[4,8,768]{2,1,0:T(8,128)} %get-tuple-element.5.sums_ref, ...), custom_call_target="tpu_custom_call" | custom-call | tf_op jit(solution)/shard_map/splice/pallas_call | solution.py:572

commit v2 on v1

--- a/solution.py
+++ b/solution.py
@@ -15,7 +15,7 @@
 D = 8192
 CH = 256
 NCH = 5
-HEAD = 192
+HEADS = (128, 208)
 SQRT_HALF = 0.7071067811865476
 
 
@@ -32,6 +32,11 @@
         device_id=device,
         device_id_type=MESH,
     ).start()
+
+
+def loop(name, count, step):
+    with jax.named_scope(name):
+        lax.fori_loop(0, count, step, 0)
 
 
 def row_squares(values):
@@ -63,6 +68,7 @@
     mer,
     hid,
     wbuf,
+    stage,
     text,
     dsend,
     drecv,
@@ -74,6 +80,7 @@
     sbuf,
     lsem,
     s0,
+    s_stage,
     s_swap,
     s_w,
     s_h,
@@ -117,25 +124,15 @@
     dev_cut = (z * 8 + y * 2 + 1 - xl, (1 - xh) * 2 + c)
     dev_core = (d, xh * 2 + 1 - c)
 
+    @pl.when(xh == 0)
+    def _():
+        pltpu.make_async_copy(w2_hbm, wbuf.at[z * 2], s_stage).start()
+
+    @pl.when(xh == 1)
+    def _():
+        pltpu.make_async_copy(w2_hbm, stage, s_stage).start()
+
     pltpu.make_async_copy(pat_hbm, pat, lsem.at[NCH]).start()
-
-    def w1_copy(n):
-        return pltpu.make_async_copy(
-            w1_hbm.at[:, pl.ds(n * CH, CH)], w1.at[n], lsem.at[n]
-        )
-
-    w1_copy(0).start()
-
-    @pl.when(xh == 0)
-    def _():
-        for kc in range(NCH):
-            pltpu.make_async_copy(
-                w2_hbm.at[pl.ds(kc * CH, CH)], wbuf.at[z * 2, kc], s0.at[kc]
-            ).start()
-
-    for n in range(1, NCH):
-        w1_copy(n).start()
-    pltpu.make_async_copy(text_hbm, text, lsem.at[NCH + 1]).start()
 
     barrier = pltpu.get_barrier_semaphore()
     base = d - lax.rem(d, 4)
@@ -155,44 +152,25 @@
     greet(dev_cut)
     for i in range(1, 4):
         greet((d, lax.rem(t + i, 4)))
-    pl.semaphore_wait(barrier, 17)
-
-    def own_send(kc):
-        block = wbuf.at[z * 2, kc]
-        wait_for(block, s0.at[kc])
-        send(block, block, s_w, r_om.at[kc], dev_zp)
-        send(block, block, s_w, r_op.at[kc], dev_zm)
-        send(block, wbuf.at[z * 2 + 1, kc], s_w, r_p.at[kc], dev_ya)
-
-    @pl.when(xh == 1)
-    def _():
-        for kc in range(NCH):
-            send(
-                w2_hbm.at[pl.ds(kc * CH, CH)],
-                wbuf.at[z * 2, kc],
-                s_swap,
-                s0.at[kc],
-                dev_x,
-            )
-
-    @pl.when(xh == 0)
-    def _():
-        for kc in range(NCH):
-            own_send(kc)
-
-    wait_for(pat, lsem.at[NCH])
-    gain = gain_ref[...]
-    nbias = nbias_ref[...]
+
     width = pat.shape[1]
-
-    def norm_step(step, carry):
+    gain = gain_ref[...].reshape(1, width)
+    nbias = nbias_ref[...].reshape(1, width)
+
+    def norm_pair(pair, carry):
+        for u in range(2):
+            norm_step(pair * 2 + u, nbuf.at[u])
+        return carry
+
+    def norm_step(step, nbuf):
         slot = lax.div(step, 4)
         part = lax.rem(step, 4)
-        values = jnp.zeros((64, width), F32)
+        values = jnp.zeros((64, width), BF16)
         for b in range(4):
             start = pl.multiple_of(b * (4 * CAP) + part * 64, 64)
-            chosen = (routing_ref[d, b] == slot).astype(F32)
-            values = values + pat[pl.ds(start, 64), :].astype(F32) * chosen
+            chosen = (routing_ref[b, d] == slot).astype(F32).astype(BF16)
+            values = values + pat[pl.ds(start, 64), :] * chosen
+        values = values.astype(F32)
         centered = values - jnp.mean(values, axis=-1, keepdims=True)
         variance = jnp.mean(centered * centered, axis=-1, keepdims=True)
         normed = centered * lax.rsqrt(variance + 1e-06) * gain + nbias
@@ -204,52 +182,223 @@
                 mer[pl.ds(row, 16), j * width + i * 128 : j * width + (i + 1) * 128] = (
                     nbuf[i, pl.ds(j, 16, stride=4), :].astype(BF16)
                 )
-        return carry
-
-    lax.fori_loop(0, 16, norm_step, 0)
+
+    with jax.named_scope("patches_in"):
+        wait_for(pat, lsem.at[NCH])
+    for n in range(NCH):
+        pltpu.make_async_copy(
+            w1_hbm.at[:, pl.ds(n * CH, CH)], w1.at[n], lsem.at[n]
+        ).start()
+    with jax.named_scope("norm_first"):
+        lax.fori_loop(0, 2, norm_pair, 0)
+    with jax.named_scope("greeting"):
+        pl.semaphore_wait(barrier, 17)
+
+    def own_send(kc):
+        block = wbuf.at[z * 2, kc]
+        send(block, block, s_w, r_om.at[kc], dev_zp)
+        send(block, block, s_w, r_op.at[kc], dev_zm)
+        send(block, wbuf.at[z * 2 + 1, kc], s_w, r_p.at[kc], dev_ya)
+
+    with jax.named_scope("second_in"):
+        wait_for(stage, s_stage)
+
+    def swapped_send(kc):
+        with jax.named_scope("swapped"):
+            wait_for(wbuf.at[z * 2, kc], s0.at[kc])
+        own_send(kc)
+
+    @pl.when(xh == 1)
+    def _():
+        for kc in range(NCH):
+            send(stage.at[kc], wbuf.at[z * 2, kc], s_swap, s0.at[kc], dev_x)
+
+    @pl.when(xh == 0)
+    def _():
+        for kc in range(3):
+            own_send(kc)
+
+    with jax.named_scope("norm_rest"):
+        lax.fori_loop(2, 8, norm_pair, 0)
+
+    @pl.when(xh == 0)
+    def _():
+        own_send(3)
+        own_send(4)
+
+    @pl.when(xh == 1)
+    def _():
+        swapped_send(0)
 
     def hidden_step(n, carry):
         wait_for(w1.at[n], lsem.at[n])
         value = jnp.dot(mer[...], w1[n], preferred_element_type=F32)
-        value = value + b1_ref[pl.ds(n, 1), :]
+        value = value + b1_ref[pl.ds(pl.multiple_of(n * CH, CH), CH)].reshape(1, CH)
         value = 0.5 * value * (1.0 + lax.erf(value * SQRT_HALF))
         hid[0, n] = value.astype(BF16)
         send(hid.at[0, n], hid.at[1, n], s_h, r_h1.at[n], dev_x)
         send(hid.at[0, n], hid.at[2, n], s_h, r_h2.at[n], dev_yb)
 
-        @pl.when((xh == 1) & (lax.rem(n, 2) == 0))
+        @pl.when((xh == 1) & ((n == 1) | (n == 4)))
         def _():
-            own_send(lax.div(n, 2))
+            swapped_send(lax.div(n, 4) + 1)
 
         return carry
 
-    lax.fori_loop(0, NCH, hidden_step, 0)
-
-    def relay_far(kc, carry):
-        @pl.when((xh == 1) & (kc < 2))
-        def _():
-            own_send(kc + 3)
-
+    loop("hidden_step", NCH, hidden_step)
+
+    pltpu.make_async_copy(text_hbm, text, lsem.at[NCH + 1]).start()
+
+    def far(kc):
         wait_for(wbuf.at[zm * 2, kc], r_om.at[kc])
         upper = wbuf.at[zm * 2, kc, pl.ds(0, CH // 2)]
         send(upper, upper, s_w, r_fm.at[kc], dev_zp)
         wait_for(wbuf.at[zp * 2, kc], r_op.at[kc])
         under = wbuf.at[zp * 2, kc, pl.ds(CH // 2, CH // 2)]
         send(under, under, s_w, r_fp.at[kc], dev_zm)
-        return carry
-
-    lax.fori_loop(0, NCH, relay_far, 0)
-
-    def relay_pair(kc, carry):
+        if kc == 0:
+            send(wbuf.at[zm * 2, 0], wbuf.at[zm * 2 + 1, 0], s_w, r_pm, dev_ya)
+            send(wbuf.at[zp * 2, 0], wbuf.at[zp * 2 + 1, 0], s_w, r_pp, dev_ya)
+
+    def late_own(kc):
+        @pl.when(xh == 1)
+        def _():
+            swapped_send(kc)
+
+    def pair(kc):
         block = wbuf.at[z * 2 + 1, kc]
         wait_for(block, r_p.at[kc])
-        send(block, block, s_w, r_pm, dev_zp)
-        send(block, block, s_w, r_pp, dev_zm)
-        return carry
-
-    lax.fori_loop(0, NCH, relay_pair, 0)
-
-    wait_for(text, lsem.at[NCH + 1])
+        if kc > 0:
+            send(block, block, s_w, r_pm, dev_zp)
+            send(block, block, s_w, r_pp, dev_zm)
+
+    def rows_x(n):
+        wait_for(hid.at[1, n], r_h1.at[n])
+        for half in range(2):
+
+            @pl.when(xh == half)
+            def _():
+                top = pl.ds(0, HEADS[half])
+                send(hid.at[1, n, top], hid.at[3, n, top], s_h, r_h3, dev_yb)
+
+    def rows_y(n):
+        wait_for(hid.at[2, n], r_h2.at[n])
+        for half in range(2):
+
+            @pl.when(xh == half)
+            def _():
+                rest = pl.ds(HEADS[half], CH - HEADS[half])
+                send(hid.at[2, n, rest], hid.at[3, n, rest], s_h, r_h3, dev_x)
+
+    def across_y(n):
+        wait_for(wbuf.at[zo * 2, n, pl.ds(0, CH // 2)], r_fm.at[n])
+        wait_for(wbuf.at[zo * 2, n, pl.ds(CH // 2, CH // 2)], r_fp.at[n])
+        send(wbuf.at[zo * 2, n], wbuf.at[zo * 2 + 1, n], s_w, r_p2, dev_ya)
+
+    def tile(rows, group, p):
+        count = len(rows) * CH
+        left = jnp.concatenate(
+            [hid[rows[0] : rows[-1] + 1, n].reshape(count, CH) for n in range(NCH)],
+            axis=1,
+        )
+        right = wbuf[group * 2 + p].reshape(NCH * CH, CH)
+        return jnp.dot(left, right, preferred_element_type=F32)
+
+    swap = lax.rem(z + c, 2)
+
+    def pick(a, b, first):
+        return a * first + b * (1 - first)
+
+    def column_of(p):
+        return (y + p * (3 - 2 * y)) * 2 + q
+
+    def tiles(same, opposite):
+        if same is None or opposite is None:
+            to_z, to_p = my_z, my_p = opposite if same is None else same
+        else:
+            to_z = pick(same[0], opposite[0], swap)
+            to_p = pick(same[1], opposite[1], swap)
+            my_z = pick(opposite[0], same[0], swap)
+            my_p = pick(opposite[1], same[1], swap)
+        to_half = lax.rem(lax.div(to_z, 2) + xh + 1, 2)
+        my_half = lax.rem(lax.div(my_z, 2) + xh + 1, 2)
+
+        def give(rows):
+            value = tile(rows, to_z, to_p).astype(BF16)
+
+            def out():
+                for i, r in enumerate(rows):
+                    dsend[to_half, to_p, r] = value[i * CH : (i + 1) * CH]
+                    send(
+                        dsend.at[to_half, to_p, r],
+                        drecv.at[to_half, to_p, r],
+                        s_d,
+                        r_d.at[to_half * 8 + to_p * 4 + r],
+                        dev_core,
+                    )
+
+            return out
+
+        def take(rows):
+            value = tile(rows, my_z, my_p)
+
+            def out():
+                for i, r in enumerate(rows):
+                    wait_for(
+                        drecv.at[my_half, my_p, r], r_d.at[my_half * 8 + my_p * 4 + r]
+                    )
+                    mine = value[i * CH : (i + 1) * CH]
+                    mine = mine + drecv[my_half, my_p, r].astype(F32)
+
+                    @pl.when(my_half == 0)
+                    def _():
+                        xsend[my_p, r] = mine.astype(BF16)
+                        there = r + 1 - 2 * (r % 2)
+                        send(
+                            xsend.at[my_p, r],
+                            xrecv.at[my_p, there],
+                            s_x,
+                            r_x.at[my_p * 4 + there],
+                            dev_cut,
+                        )
+
+                    @pl.when(my_half == 1)
+                    def _():
+                        column = pl.multiple_of(column_of(my_p) * CH, CH)
+                        fbuf[my_p, r] = mine + b2_ref[:, pl.ds(column, CH)]
+
+            return out
+
+        return give, take
+
+    near_a = tiles((z, 0), (zm, 0))
+    near_b = tiles((z, 1), (zp, 0))
+    middle = tiles((zo, 0), None)
+    far_a = tiles((zo, 1), (zm, 1))
+    far_b = tiles(None, (zp, 1))
+
+    def give_near(r):
+        with jax.named_scope(f"give_near{r}"):
+            outs = [near_a[0]([r]), near_b[0]([r])]
+            for out in outs:
+                out()
+
+    def take_near(r):
+        with jax.named_scope(f"take_near{r}"):
+            outs = [near_a[1]([r]), near_b[1]([r])]
+            for out in outs:
+                out()
+
+    def run_single(name, steps, mine, rows):
+        with jax.named_scope(name):
+
+            @pl.when(swap != mine)
+            def _():
+                steps[0](rows)()
+
+            @pl.when(swap == mine)
+            def _():
+                steps[1](rows)()
 
     def text_step(i, carry):
         rows = pl.ds(pl.multiple_of(i * CH, CH), CH)
@@ -260,95 +409,52 @@
         sbuf[t, :, rows] = row_squares(total)
         return carry
 
-    lax.fori_loop(0, 2, text_step, 0)
-
-    def relay_rows(n, carry):
-        wait_for(hid.at[1, n], r_h1.at[n])
-        send(
-            hid.at[1, n, pl.ds(0, HEAD)],
-            hid.at[3, n, pl.ds(0, HEAD)],
-            s_h,
-            r_h3,
-            dev_yb,
-        )
-        wait_for(hid.at[2, n], r_h2.at[n])
-        send(
-            hid.at[2, n, pl.ds(HEAD, CH - HEAD)],
-            hid.at[3, n, pl.ds(HEAD, CH - HEAD)],
-            s_h,
-            r_h3,
-            dev_x,
-        )
-        wait_for(wbuf.at[zo * 2, n, pl.ds(0, CH // 2)], r_fm.at[n])
-        wait_for(wbuf.at[zo * 2, n, pl.ds(CH // 2, CH // 2)], r_fp.at[n])
-        send(wbuf.at[zo * 2, n], wbuf.at[zo * 2 + 1, n], s_w, r_p2, dev_ya)
-        return carry
-
-    lax.fori_loop(0, NCH, relay_rows, 0)
-    wait_for(hid.at[3], r_h3)
-
-    def tile(r, group, p):
-        total = jnp.dot(hid[r, 0], wbuf[group * 2 + p, 0], preferred_element_type=F32)
-        for n in range(1, NCH):
-            total = total + jnp.dot(
-                hid[r, n], wbuf[group * 2 + p, n], preferred_element_type=F32
-            )
-        return total
-
-    other = (1 - xh) * 2
-    mine = xh * 2
-
-    def to_core(half, p, group):
-        def step(r, carry):
-            dsend[half, p, r] = tile(r, group, p).astype(BF16)
-            send(
-                dsend.at[half, p, r],
-                drecv.at[half, p, r],
-                s_d,
-                r_d.at[half * 8 + p * 4 + r],
-                dev_core,
-            )
-            return carry
-
-        lax.fori_loop(0, 4, step, 0)
-
-    def across(p):
-        def step(r, carry):
-            value = tile(r, other + c, p)
-            wait_for(drecv.at[0, p, r], r_d.at[p * 4 + r])
-            value = value + drecv[0, p, r].astype(F32)
-            xsend[p, r] = value.astype(BF16)
-            there = r + 1 - 2 * lax.rem(r, 2)
-            send(
-                xsend.at[p, r], xrecv.at[p, there], s_x, r_x.at[p * 4 + there], dev_cut
-            )
-            return carry
-
-        lax.fori_loop(0, 4, step, 0)
-
-    def keep(p):
-        column = pl.multiple_of((y + p * (3 - 2 * y)) * 512 + q * CH, CH)
-        bias = b2_ref[:, pl.ds(column, CH)]
-
-        def step(r, carry):
-            value = tile(r, mine + c, p)
-            wait_for(drecv.at[1, p, r], r_d.at[8 + p * 4 + r])
-            fbuf[p, r] = value + drecv[1, p, r].astype(F32) + bias
-            return carry
-
-        lax.fori_loop(0, 4, step, 0)
-
-    to_core(0, 0, other + 1 - c)
-    across(0)
-    wait_for(wbuf.at[zm * 2 + 1], r_pm)
-    wait_for(wbuf.at[zp * 2 + 1], r_pp)
-    wait_for(wbuf.at[zo * 2 + 1], r_p2)
-    to_core(0, 1, other + 1 - c)
-    across(1)
-    to_core(1, 0, mine + 1 - c)
-    to_core(1, 1, mine + 1 - c)
-    keep(0)
-    keep(1)
+    def step(label, work, *args):
+        with jax.named_scope(label):
+            work(*args)
+
+    step("rows_y0", rows_y, 0)
+    late_own(3)
+    step("rows_y1", rows_y, 1)
+    late_own(4)
+    step("far0", far, 0)
+    step("far1", far, 1)
+    with jax.named_scope("text_in"):
+        wait_for(text, lsem.at[NCH + 1])
+    loop("text_step", 2, text_step)
+    step("far2", far, 2)
+    step("rows_y2", rows_y, 2)
+    step("rows_x0", rows_x, 0)
+    step("far3", far, 3)
+    step("rows_y3", rows_y, 3)
+    step("far4", far, 4)
+    step("pair01", pair, 0)
+    pair(1)
+    step("rows_x1", rows_x, 1)
+    step("rows_y4", rows_y, 4)
+    pair(2)
+    pair(3)
+    pair(4)
+    give_near(0)
+    step("across_y0", across_y, 0)
+    step("rows_x2", rows_x, 2)
+    give_near(2)
+    step("across_y1", across_y, 1)
+    take_near(0)
+    step("rows_x3", rows_x, 3)
+    step("across_y2", across_y, 2)
+    take_near(2)
+    step("across_y3", across_y, 3)
+    step("rows_x4", rows_x, 4)
+    give_near(1)
+    step("across_y4", across_y, 4)
+    run_single("middle", middle, 0, [0, 1, 2])
+    take_near(1)
+    with jax.named_scope("diagonal"):
+        wait_for(hid.at[3], r_h3)
+    give_near(3)
+    run_single("middle3", middle, 0, [3])
+    take_near(3)
 
     def target(r, k):
         row_y = y + lax.div(r, 2) * (yb - y)
@@ -357,12 +463,10 @@
 
     def pieces(p, r, k):
         rows = pl.ds(k * CAP, CAP)
-        column = (y + p * (3 - 2 * y)) * 2 + q
-        return obuf.at[p, r, rows], img.at[column, rows]
-
-    for p in range(2):
-
-        def finish(r, carry):
+        return obuf.at[p, r, rows], img.at[column_of(p), rows]
+
+    def finish(p, r):
+        with jax.named_scope(f"finish{p}{r}"):
             wait_for(xrecv.at[p, r], r_x.at[p * 4 + r])
             obuf[p, r] = (fbuf[p, r] + xrecv[p, r].astype(F32)).astype(BF16)
             for k in range(4):
@@ -377,11 +481,37 @@
                 def _():
                     send(src, dst, s_i.at[p * 16 + r * 4 + k], r_i, (e, t))
 
-            return carry
-
-        lax.fori_loop(0, 4, finish, 0)
-
-    wait_for(img, r_i)
+    def finish_early(r):
+        @pl.when(t != zo)
+        def _():
+            finish(0, r)
+
+    finish_early(1)
+    with jax.named_scope("pair_blocks"):
+        wait_for(wbuf.at[zo * 2 + 1], r_p2)
+        wait_for(wbuf.at[zm * 2 + 1], r_pm)
+    every = [0, 1, 2, 3]
+    with jax.named_scope("give_far"):
+        far_a[0](every)()
+    finish_early(3)
+    with jax.named_scope("take_far"):
+        far_a[1](every)()
+    with jax.named_scope("pair_blocks"):
+        wait_for(wbuf.at[zp * 2 + 1], r_pp)
+    run_single("far_b", far_b, 1, every)
+    finish_early(0)
+
+    @pl.when(t == zo)
+    def _():
+        for r in (1, 3, 0):
+            finish(0, r)
+
+    finish(0, 2)
+    for r in (1, 0, 3, 2):
+        finish(1, r)
+
+    with jax.named_scope("image_in"):
+        wait_for(img, r_i)
     img_copy = pltpu.make_async_copy(img, img_out, lsem.at[0])
     img_copy.start()
     total = jnp.zeros((CH, CH), F32)
@@ -397,8 +527,9 @@
             r_s.at[i - 1],
             (d, lax.rem(t + i, 4)),
         )
-    for i in range(1, 4):
-        wait_for(sbuf.at[lax.rem(t + 4 - i, 4)], r_s.at[i - 1])
+    with jax.named_scope("sums_in"):
+        for i in range(1, 4):
+            wait_for(sbuf.at[lax.rem(t + 4 - i, 4)], r_s.at[i - 1])
     sums_copy = pltpu.make_async_copy(sbuf, sums_out, lsem.at[1])
     sums_copy.start()
 
@@ -423,7 +554,7 @@
 
             return carry
 
-        lax.fori_loop(0, 4, drain, 0)
+        loop("drain", 4, drain)
     for i in range(1, 4):
         wait_for(sbuf.at[t], s_s.at[i - 1])
     img_copy.wait()
@@ -442,8 +573,8 @@
         s = lax.rem(d + SHARDS - k, SHARDS)
         count = jnp.int32(0)
         for b in range(4):
-            size = grids_ref[s, 2 * b] * grids_ref[s, 2 * b + 1]
-            count = count + jnp.where(routing_ref[s, b] == k, size, 0)
+            size = grids_ref[b, 0, s] * grids_ref[b, 1, s]
+            count = count + jnp.where(routing_ref[b, s] == k, size, 0)
         starts.append(total)
         total = total + count
     position = g * rows + lax.broadcasted_iota(jnp.int32, (rows, 1), 0)
@@ -515,10 +646,11 @@
         scratch_shapes=[
             pltpu.VMEM(patches.shape, BF16),
             pltpu.VMEM((NCH, first_weight.shape[0], CH), BF16),
-            pltpu.VMEM((width // 128, 64, 128), F32),
+            pltpu.VMEM((2, width // 128, 64, 128), F32),
             pltpu.VMEM((CH, 4 * width), BF16),
             pltpu.VMEM((4, NCH, CH, CH), BF16),
             pltpu.VMEM((8, NCH, CH, CH), BF16),
+            pltpu.VMEM((NCH, CH, CH), BF16),
             pltpu.VMEM((seq, features), BF16),
             pltpu.VMEM((2, 2, 4, CH, CH), BF16),
             pltpu.VMEM((2, 2, 4, CH, CH), BF16),
@@ -535,6 +667,7 @@
             dma,
             dma,
             dma,
+            dma,
             dma((32,)),
             dma((3,)),
             dma((NCH,)),
@@ -558,13 +691,13 @@
         ),
         name="merge",
     )(
-        routing,
+        routing.T,
         patches,
-        norm_gain.reshape(1, -1),
-        norm_bias.reshape(1, -1),
+        norm_gain,
+        norm_bias,
         first_weight,
-        first_bias.reshape(NCH, CH),
-        second_weight,
+        first_bias,
+        second_weight.reshape(NCH, CH, CH),
         second_bias.reshape(1, -1),
         text_embeds,
     )
@@ -590,8 +723,8 @@
         ),
         name="splice",
     )(
-        image_grids.reshape(SHARDS, -1),
-        routing,
+        image_grids.transpose(1, 2, 0),
+        routing.T,
         text_embeds,
         img,
         sums,

time: 101 us -> 84.9 us (0.84)
  the two profiles are of different devices: /device:TPU:1 before, /device:TPU:33 now
where the time goes in v2:
time: 84.9 us; the launch traced here: 84.7 us
  Pallas kernels  84 us (99%)
    pallas_call x1, Pallas kernels, per_device(): pl.pallas_call(merge_kernel, out_shape=(jax.ShapeDtypeStruct((8, CH, CH),...  78.6 us
    pallas_call x1, Pallas kernels, per_device(): pl.pallas_call(splice_kernel, grid=(seq // rows,), out_shape=(jax.ShapeDt...  5.49 us

profile of v2, /device:TPU:33, one launch (start us, length us, event | category | flops | bytes accessed | tf_op | source)
XLA Modules:
  0.0 84.7 jit_solution(10733366772296058574)
XLA Ops:
  0.6 78.6 %merge.1 = (bf16[8,256,256]{2,1,0:T(8,128)(2,1)}, f32[4,8,768]{2,1,0:T(8,128)}) custom-call(s32[4,32]{1,0:T(4,128)} %bitcast.8, bf16[1024,1280]{1,0:T(8,128)(2,1)} %pat_hbm.1, f32[1280]{0:T(1024)} %gain_ref.1, f32[1280]{0:T(1024)} %nbias_ref.1, bf16[5120,1280]{1,0:T(8,128)(2,1)} %w1_hbm.1, f32[1280]{0:T(1024)} %b1_ref.1, bf16[5,256,256]{2,1,0:T(8,128)(2,1)} %bitcast.5, ...), custom_call_target="tpu_custom_call" | custom-call | tf_op jit(solution)/shard_map/merge/pallas_call | solution.py:638
  79.2 5.5 %splice.1 = (bf16[512,2048]{1,0:T(8,128)(2,1)}, bf16[512,2048]{1,0:T(8,128)(2,1)}) custom-call(s32[4,2,32]{2,1,0:T(2,128)} %bitcast.10, s32[4,32]{1,0:T(4,128)} %bitcast.9, bf16[512,2048]{1,0:T(8,128)(2,1)} %text_ref.1, bf16[8,256,256]{2,1,0:T(8,128)(2,1)} %get-tuple-element.4.img_ref, f32[4,8,768]{2,1,0:T(8,128)} %get-tuple-element.5.sums_ref, ...), custom_call_target="tpu_custom_call" | custom-call | tf_op jit(solution)/shard_map/splice/pallas_call | solution.py:705

commit v3 on v2

--- a/solution.py
+++ b/solution.py
@@ -51,17 +51,23 @@
 
 
 def merge_kernel(
+    routing_hbm,
+    pat_hbm,
+    gain_hbm,
+    nbias_hbm,
+    w1_hbm,
+    b1_hbm,
+    w2_hbm,
+    b2_hbm,
+    text_hbm,
+    img_out,
+    tsums_out,
+    isums_out,
     routing_ref,
-    pat_hbm,
     gain_ref,
     nbias_ref,
-    w1_hbm,
     b1_ref,
-    w2_hbm,
     b2_ref,
-    text_hbm,
-    img_out,
-    sums_out,
     pat,
     w1,
     nbuf,
@@ -77,9 +83,12 @@
     fbuf,
     obuf,
     img,
-    sbuf,
+    tbuf,
+    ibuf,
     lsem,
+    s_small,
     s0,
+    s_first,
     s_stage,
     s_swap,
     s_w,
@@ -87,6 +96,7 @@
     s_d,
     s_x,
     s_i,
+    s_t,
     s_s,
     r_om,
     r_op,
@@ -102,6 +112,7 @@
     r_d,
     r_x,
     r_i,
+    r_t,
     r_s,
 ):
     d = lax.axis_index("dp")
@@ -134,6 +145,21 @@
 
     pltpu.make_async_copy(pat_hbm, pat, lsem.at[NCH]).start()
 
+    small = [
+        pltpu.make_async_copy(src, dst, s_small.at[i])
+        for i, (src, dst) in enumerate(
+            (
+                (routing_hbm, routing_ref),
+                (gain_hbm, gain_ref),
+                (nbias_hbm, nbias_ref),
+                (b1_hbm, b1_ref),
+                (b2_hbm, b2_ref),
+            )
+        )
+    ]
+    for copy in small:
+        copy.start()
+
     barrier = pltpu.get_barrier_semaphore()
     base = d - lax.rem(d, 4)
 
@@ -152,6 +178,9 @@
     greet(dev_cut)
     for i in range(1, 4):
         greet((d, lax.rem(t + i, 4)))
+
+    for copy in small:
+        copy.wait()
 
     width = pat.shape[1]
     gain = gain_ref[...].reshape(1, width)
@@ -194,14 +223,21 @@
     with jax.named_scope("greeting"):
         pl.semaphore_wait(barrier, 17)
 
-    def own_send(kc):
-        block = wbuf.at[z * 2, kc]
+    def own_send(kc, part=pl.ds(0, CH)):
+        block = wbuf.at[z * 2, kc, part]
         send(block, block, s_w, r_om.at[kc], dev_zp)
         send(block, block, s_w, r_op.at[kc], dev_zm)
-        send(block, wbuf.at[z * 2 + 1, kc], s_w, r_p.at[kc], dev_ya)
+        send(block, wbuf.at[z * 2 + 1, kc, part], s_w, r_p.at[kc], dev_ya)
 
     with jax.named_scope("second_in"):
         wait_for(stage, s_stage)
+
+    halves = (pl.ds(0, CH // 2), pl.ds(CH // 2, CH // 2))
+
+    def swapped_half(half):
+        with jax.named_scope("swapped"):
+            wait_for(wbuf.at[z * 2, 0, halves[half]], s_first.at[half])
+        own_send(0, halves[half])
 
     def swapped_send(kc):
         with jax.named_scope("swapped"):
@@ -210,7 +246,15 @@
 
     @pl.when(xh == 1)
     def _():
-        for kc in range(NCH):
+        for half in range(2):
+            send(
+                stage.at[0, halves[half]],
+                wbuf.at[z * 2, 0, halves[half]],
+                s_swap,
+                s_first.at[half],
+                dev_x,
+            )
+        for kc in range(1, NCH):
             send(stage.at[kc], wbuf.at[z * 2, kc], s_swap, s0.at[kc], dev_x)
 
     @pl.when(xh == 0)
@@ -228,7 +272,7 @@
 
     @pl.when(xh == 1)
     def _():
-        swapped_send(0)
+        swapped_half(0)
 
     def hidden_step(n, carry):
         wait_for(w1.at[n], lsem.at[n])
@@ -239,9 +283,13 @@
         send(hid.at[0, n], hid.at[1, n], s_h, r_h1.at[n], dev_x)
         send(hid.at[0, n], hid.at[2, n], s_h, r_h2.at[n], dev_yb)
 
-        @pl.when((xh == 1) & ((n == 1) | (n == 4)))
+        @pl.when((xh == 1) & (n == 0))
         def _():
-            swapped_send(lax.div(n, 4) + 1)
+            swapped_half(1)
+
+        @pl.when((xh == 1) & ((n == 2) | (n == 4)))
+        def _():
+            swapped_send(lax.div(n, 2))
 
         return carry
 
@@ -374,8 +422,10 @@
     near_a = tiles((z, 0), (zm, 0))
     near_b = tiles((z, 1), (zp, 0))
     middle = tiles((zo, 0), None)
-    far_a = tiles((zo, 1), (zm, 1))
-    far_b = tiles(None, (zp, 1))
+    up = lax.rem(lax.div(zp, 2) + xh, 2)
+    far_a = tiles((zo, 1), None)
+    far_b = tiles(None, (pick(zp, zm, up), 1))
+    far_c = tiles(None, (pick(zm, zp, up), 1))
 
     def give_near(r):
         with jax.named_scope(f"give_near{r}"):
@@ -406,8 +456,18 @@
         for j in range(8):
             values = text[rows, j * CH : (j + 1) * CH].astype(F32)
             total = total + values * values
-        sbuf[t, :, rows] = row_squares(total)
+        tbuf[t, :, rows] = row_squares(total)
         return carry
+
+    def share(buf, send_sems, recv_sems):
+        for i in range(1, 4):
+            send(
+                buf.at[t],
+                buf.at[t],
+                send_sems.at[i - 1],
+                recv_sems.at[i - 1],
+                (d, lax.rem(t + i, 4)),
+            )
 
     def step(label, work, *args):
         with jax.named_scope(label):
@@ -422,6 +482,7 @@
     with jax.named_scope("text_in"):
         wait_for(text, lsem.at[NCH + 1])
     loop("text_step", 2, text_step)
+    share(tbuf, s_t, r_t)
     step("far2", far, 2)
     step("rows_y2", rows_y, 2)
     step("rows_x0", rows_x, 0)
@@ -477,38 +538,52 @@
                 def _():
                     pltpu.make_async_copy(src, dst, r_i).start()
 
-                @pl.when(e != d)
+                @pl.when((e != d) & (lax.div(e, 4) == lax.div(d, 4)))
                 def _():
                     send(src, dst, s_i.at[p * 16 + r * 4 + k], r_i, (e, t))
 
-    def finish_early(r):
-        @pl.when(t != zo)
+    def onward(p, r):
+        for k in range(1, 4):
+            e = target(r, k)
+            src, dst = pieces(p, r, k)
+
+            @pl.when(lax.div(e, 4) != lax.div(d, 4))
+            def _():
+                send(src, dst, s_i.at[p * 16 + r * 4 + k], r_i, (e, t))
+
+    def on_side(side, *work):
+        @pl.when(xh == side)
         def _():
-            finish(0, r)
-
-    finish_early(1)
+            for do, p, rows in work:
+                for r in rows:
+                    do(p, r)
+
+    @pl.when((xh == 0) & (t != zo))
+    def _():
+        finish(0, 1)
+
+    on_side(1, (finish, 0, (1, 3, 0, 2)))
+    every = [0, 1, 2, 3]
+    with jax.named_scope("pair_blocks_o"):
+        wait_for(wbuf.at[zo * 2 + 1], r_p2)
+    run_single("far_a", far_a, 0, every)
+
+    @pl.when((xh == 0) & (t == zo))
+    def _():
+        finish(0, 1)
+
+    on_side(0, (onward, 0, (1,)), (finish, 0, (3,)), (onward, 0, (3,)))
+    on_side(1, (onward, 0, (1, 3, 0, 2)))
     with jax.named_scope("pair_blocks"):
-        wait_for(wbuf.at[zo * 2 + 1], r_p2)
         wait_for(wbuf.at[zm * 2 + 1], r_pm)
-    every = [0, 1, 2, 3]
-    with jax.named_scope("give_far"):
-        far_a[0](every)()
-    finish_early(3)
-    with jax.named_scope("take_far"):
-        far_a[1](every)()
-    with jax.named_scope("pair_blocks"):
         wait_for(wbuf.at[zp * 2 + 1], r_pp)
     run_single("far_b", far_b, 1, every)
-    finish_early(0)
-
-    @pl.when(t == zo)
-    def _():
-        for r in (1, 3, 0):
-            finish(0, r)
-
-    finish(0, 2)
+    on_side(0, (finish, 0, (0,)), (onward, 0, (0,)))
+    run_single("far_c", far_c, 1, every)
+    on_side(0, (finish, 0, (2,)), (onward, 0, (2,)))
     for r in (1, 0, 3, 2):
         finish(1, r)
+        onward(1, r)
 
     with jax.named_scope("image_in"):
         wait_for(img, r_i)
@@ -518,19 +593,16 @@
     for b in range(8):
         values = img[b].astype(F32)
         total = total + values * values
-    sbuf[t, :, pl.ds(512, CH)] = row_squares(total)
+    ibuf[t] = row_squares(total)
+    share(ibuf, s_s, r_s)
     for i in range(1, 4):
-        send(
-            sbuf.at[t],
-            sbuf.at[t],
-            s_s.at[i - 1],
-            r_s.at[i - 1],
-            (d, lax.rem(t + i, 4)),
-        )
+        wait_for(tbuf.at[lax.rem(t + 4 - i, 4)], r_t.at[i - 1])
+    text_copy = pltpu.make_async_copy(tbuf, tsums_out, lsem.at[2])
+    text_copy.start()
     with jax.named_scope("sums_in"):
         for i in range(1, 4):
-            wait_for(sbuf.at[lax.rem(t + 4 - i, 4)], r_s.at[i - 1])
-    sums_copy = pltpu.make_async_copy(sbuf, sums_out, lsem.at[1])
+            wait_for(ibuf.at[lax.rem(t + 4 - i, 4)], r_s.at[i - 1])
+    sums_copy = pltpu.make_async_copy(ibuf, isums_out, lsem.at[1])
     sums_copy.start()
 
     wait_for(wbuf.at[pl.ds(0, 7)], s_w)
@@ -556,17 +628,63 @@
 
         loop("drain", 4, drain)
     for i in range(1, 4):
-        wait_for(sbuf.at[t], s_s.at[i - 1])
+        wait_for(tbuf.at[t], s_t.at[i - 1])
+        wait_for(ibuf.at[t], s_s.at[i - 1])
     img_copy.wait()
+    text_copy.wait()
     sums_copy.wait()
 
 
 def splice_kernel(
-    grids_ref, routing_ref, text_ref, img_ref, sums_ref, gain_ref, emb_ref, out_ref
+    grids_ref,
+    routing_ref,
+    text_hbm,
+    img_hbm,
+    tsums_hbm,
+    isums_hbm,
+    gain_hbm,
+    emb_hbm,
+    out_hbm,
+    text,
+    img,
+    tsums,
+    isums,
+    gain,
+    emb,
+    out,
+    in_sem,
+    emb_sem,
+    out_sem,
 ):
+    rows = 128
+    images = 4 * CAP
+    steps = text.shape[0] // rows
+    first = images // rows
+
+    def part(ref, i):
+        return ref.at[pl.ds(i * rows, rows)]
+
+    small = [
+        pltpu.make_async_copy(tsums_hbm, tsums, in_sem.at[steps]),
+        pltpu.make_async_copy(isums_hbm, isums, in_sem.at[steps + 1]),
+        pltpu.make_async_copy(gain_hbm, gain, in_sem.at[steps + 2]),
+    ]
+    whole = pltpu.make_async_copy(img_hbm, img, in_sem.at[steps + 3])
+    order = list(range(first, steps)) + list(range(first))
+    loads = {
+        i: pltpu.make_async_copy(part(text_hbm, i), part(text, i), in_sem.at[i])
+        for i in order
+    }
+    for copy in small[:1] + small[2:]:
+        copy.start()
+    for i in order[: steps - first]:
+        loads[i].start()
+    whole.start()
+    small[1].start()
+    for i in order[steps - first :]:
+        loads[i].start()
+
     d = lax.axis_index("dp")
-    g = pl.program_id(0)
-    rows = text_ref.shape[0]
     starts = []
     total = jnp.int32(0)
     for k in range(4):
@@ -577,43 +695,62 @@
             count = count + jnp.where(routing_ref[b, s] == k, size, 0)
         starts.append(total)
         total = total + count
-    position = g * rows + lax.broadcasted_iota(jnp.int32, (rows, 1), 0)
-    source = position
-    for k in range(1, 4):
-        begin = jnp.where(position >= starts[k], k * CAP - starts[k], 0)
-        if k > 1:
-            begin = begin - jnp.where(
-                position >= starts[k], (k - 1) * CAP - starts[k - 1], 0
+
+    def picked(sums_ref, index):
+        sums = sums_ref[0] + sums_ref[1] + sums_ref[2] + sums_ref[3]
+        sums = sums[0:1, :]
+        lanes = lax.broadcasted_iota(jnp.int32, (rows, sums.shape[1]), 1)
+        return jnp.sum(jnp.where(lanes == index, sums, 0.0), axis=-1, keepdims=True)
+
+    copies = []
+    for copy in small[:1] + small[2:]:
+        copy.wait()
+    for i in order:
+        position = i * rows + lax.broadcasted_iota(jnp.int32, (rows, 1), 0)
+        square = picked(tsums, position)
+        loads[i].wait()
+        if i >= first:
+            copies.append(
+                pltpu.make_async_copy(part(text, i), part(emb_hbm, i), emb_sem.at[i])
             )
-        source = source + begin
-    live = position < total
-    sums = sums_ref[0] + sums_ref[1] + sums_ref[2] + sums_ref[3]
-    sums = sums[0:1, :]
-    index = jnp.where(live, 512 + source, position)
-    lanes = lax.broadcasted_iota(jnp.int32, (rows, sums.shape[1]), 1)
-    square = jnp.sum(jnp.where(lanes == index, sums, 0.0), axis=-1, keepdims=True)
-    scale = lax.rsqrt(square / D + 1e-06)
-    picks = jnp.where(
-        lax.broadcasted_iota(jnp.int32, (rows, 4 * CAP), 1) == source, 1.0, 0.0
-    ).astype(BF16)
-    blocks = img_ref.shape[0]
-
-    @pl.when(g * rows < 4 * CAP)
-    def _():
-        for b in range(blocks):
+            copies[-1].start()
+            scale = lax.rsqrt(square / D + 1e-06)
+        else:
+            if i == 0:
+                whole.wait()
+                small[1].wait()
+            source = position
+            for k in range(1, 4):
+                shift = k * CAP - starts[k]
+                if k > 1:
+                    shift = shift - ((k - 1) * CAP - starts[k - 1])
+                source = source + jnp.where(position >= starts[k], shift, 0)
+            live = position < total
+            square = jnp.where(live, picked(isums, source), square)
+            scale = lax.rsqrt(square / D + 1e-06)
+            picks = jnp.where(
+                lax.broadcasted_iota(jnp.int32, (rows, images), 1) == source, 1.0, 0.0
+            ).astype(BF16)
+        here = slice(i * rows, (i + 1) * rows)
+        for b in range(img.shape[0]):
             cols = slice(b * CH, (b + 1) * CH)
-            taken = jnp.dot(picks, img_ref[b], preferred_element_type=F32)
-            value = jnp.where(live, taken, text_ref[:, cols].astype(F32))
-            emb_ref[:, cols] = value.astype(BF16)
-            out_ref[:, cols] = (value * scale * gain_ref[:, cols]).astype(BF16)
-
-    @pl.when(g * rows >= 4 * CAP)
-    def _():
-        for b in range(blocks):
-            cols = slice(b * CH, (b + 1) * CH)
-            value = text_ref[:, cols].astype(F32)
-            emb_ref[:, cols] = text_ref[:, cols]
-            out_ref[:, cols] = (value * scale * gain_ref[:, cols]).astype(BF16)
+            value = text[here, cols].astype(F32)
+            if i < first:
+                taken = jnp.dot(picks, img[b], preferred_element_type=F32)
+                value = jnp.where(live, taken, value)
+                emb[here, cols] = value.astype(BF16)
+            out[here, cols] = (value * scale * gain[:, cols]).astype(BF16)
+        if i < first:
+            copies.append(
+                pltpu.make_async_copy(part(emb, i), part(emb_hbm, i), emb_sem.at[i])
+            )
+            copies[-1].start()
+        copies.append(
+            pltpu.make_async_copy(part(out, i), part(out_hbm, i), out_sem.at[i])
+        )
+        copies[-1].start()
+    for copy in copies:
+        copy.wait()
 
 
 def per_device(
@@ -631,19 +768,24 @@
 ):
     seq, features = text_embeds.shape
     width = patches.shape[1]
-    hbm = pl.BlockSpec(memory_space=pl.ANY)
-    vmem = pl.BlockSpec(memory_space=pltpu.VMEM)
+    anywhere = pl.BlockSpec(memory_space=pl.ANY)
     smem = pl.BlockSpec(memory_space=pltpu.SMEM)
     dma = pltpu.SemaphoreType.DMA
-    img, sums = pl.pallas_call(
+    img, tsums, isums = pl.pallas_call(
         merge_kernel,
         out_shape=(
             jax.ShapeDtypeStruct((8, CH, CH), BF16),
-            jax.ShapeDtypeStruct((4, 8, seq + CH), F32),
+            jax.ShapeDtypeStruct((4, 8, seq), F32),
+            jax.ShapeDtypeStruct((4, 8, CH), F32),
         ),
-        in_specs=[smem, hbm, vmem, vmem, hbm, vmem, hbm, vmem, hbm],
-        out_specs=(hbm, hbm),
+        in_specs=[pl.BlockSpec(memory_space=pltpu.HBM)] * 9,
+        out_specs=(anywhere, anywhere, anywhere),
         scratch_shapes=[
+            pltpu.SMEM(routing.T.shape, jnp.int32),
+            pltpu.VMEM(norm_gain.shape, F32),
+            pltpu.VMEM(norm_bias.shape, F32),
+            pltpu.VMEM(first_bias.shape, F32),
+            pltpu.VMEM((1, second_bias.shape[0]), F32),
             pltpu.VMEM(patches.shape, BF16),
             pltpu.VMEM((NCH, first_weight.shape[0], CH), BF16),
             pltpu.VMEM((2, width // 128, 64, 128), F32),
@@ -659,9 +801,12 @@
             pltpu.VMEM((2, 4, CH, CH), F32),
             pltpu.VMEM((2, 4, CH, CH), BF16),
             pltpu.VMEM((8, CH, CH), BF16),
-            pltpu.VMEM((4, 8, seq + CH), F32),
+            pltpu.VMEM((4, 8, seq), F32),
+            pltpu.VMEM((4, 8, CH), F32),
             dma((NCH + 2,)),
+            dma((5,)),
             dma((NCH,)),
+            dma((2,)),
             dma,
             dma,
             dma,
@@ -669,6 +814,7 @@
             dma,
             dma,
             dma((32,)),
+            dma((3,)),
             dma((3,)),
             dma((NCH,)),
             dma((NCH,)),
@@ -684,6 +830,7 @@
             dma((16,)),
             dma((8,)),
             dma,
+            dma((3,)),
             dma((3,)),
         ],
         compiler_params=pltpu.CompilerParams(
@@ -701,33 +848,35 @@
         second_bias.reshape(1, -1),
         text_embeds,
     )
-    rows = 128
     return pl.pallas_call(
         splice_kernel,
-        grid=(seq // rows,),
         out_shape=(
             jax.ShapeDtypeStruct((seq, features), BF16),
             jax.ShapeDtypeStruct((seq, features), BF16),
         ),
-        in_specs=[
-            smem,
-            smem,
-            pl.BlockSpec((rows, features), lambda g: (g, 0)),
-            vmem,
-            vmem,
-            vmem,
+        in_specs=[smem, smem] + [anywhere] * 5,
+        out_specs=(anywhere, anywhere),
+        scratch_shapes=[
+            pltpu.VMEM((seq, features), BF16),
+            pltpu.VMEM(img.shape, BF16),
+            pltpu.VMEM(tsums.shape, F32),
+            pltpu.VMEM(isums.shape, F32),
+            pltpu.VMEM((1, features), F32),
+            pltpu.VMEM((4 * CAP, features), BF16),
+            pltpu.VMEM((seq, features), BF16),
+            dma((8,)),
+            dma((4,)),
+            dma((4,)),
         ],
-        out_specs=(
-            pl.BlockSpec((rows, features), lambda g: (g, 0)),
-            pl.BlockSpec((rows, features), lambda g: (g, 0)),
-        ),
+        compiler_params=pltpu.CompilerParams(vmem_limit_bytes=60 * 1024 * 1024),
         name="splice",
     )(
         image_grids.transpose(1, 2, 0),
         routing.T,
         text_embeds,
         img,
-        sums,
+        tsums,
+        isums,
         final_gain.reshape(1, -1),
     )
 

time: 84.9 us -> 82 us (0.966)
  the two profiles are of different devices: /device:TPU:33 before, /device:TPU:1 now
where the time goes in v3:
time: 82 us; the launch traced here: 81.7 us
  Pallas kernels  80.9 us (99%)
    pallas_call x1, Pallas kernels, per_device(): pl.pallas_call(merge_kernel, out_shape=(jax.ShapeDtypeStruct((8, CH, CH),...  76.6 us
    pallas_call x1, Pallas kernels, per_device(): pl.pallas_call(splice_kernel, out_shape=(jax.ShapeDtypeStruct((seq, featu...  4.33 us

profile of v3, /device:TPU:1, one launch (start us, length us, event | category | flops | bytes accessed | tf_op | source)
XLA Modules:
  0.0 81.7 jit_solution(3151028806192410619)
XLA Ops:
  0.6 76.6 %merge.1 = (bf16[8,256,256]{2,1,0:T(8,128)(2,1)}, f32[4,8,512]{2,1,0:T(8,128)}, f32[4,8,256]{2,1,0:T(8,128)}) custom-call(s32[4,32]{1,0:T(4,128)} %bitcast.8, bf16[1024,1280]{1,0:T(8,128)(2,1)} %pat_hbm.1, f32[1280]{0:T(1024)} %gain_hbm.1, f32[1280]{0:T(1024)} %nbias_hbm.1, bf16[5120,1280]{1,0:T(8,128)(2,1)} %w1_hbm.1, f32[1280]{0:T(1024)} %b1_hbm.1, ...), custom_call_target="tpu_custom_call" | custom-call | tf_op jit(solution)/shard_map/merge/pallas_call | solution.py:774
  77.2 4.3 %splice.1 = (bf16[512,2048]{1,0:T(8,128)(2,1)}, bf16[512,2048]{1,0:T(8,128)(2,1)}) custom-call(s32[4,2,32]{2,1,0:T(2,128)} %bitcast.10, s32[4,32]{1,0:T(4,128)} %bitcast.9, bf16[512,2048]{1,0:T(8,128)(2,1)} %text_hbm.3, bf16[8,256,256]{2,1,0:T(8,128)(2,1)} %get-tuple-element.5.img_hbm, f32[4,8,512]{2,1,0:T(8,128)} %get-tuple-element.6.tsums_hbm, ...), custom_call_target="tpu_custom_call" | custom-call | tf_op jit(solution)/shard_map/splice/pallas_call | solution.py:851

commit v4 on v3

--- a/solution.py
+++ b/solution.py
@@ -92,6 +92,9 @@
     s_stage,
     s_swap,
     s_w,
+    s_p,
+    s_p0,
+    s_e,
     s_h,
     s_d,
     s_x,
@@ -304,9 +307,6 @@
         wait_for(wbuf.at[zp * 2, kc], r_op.at[kc])
         under = wbuf.at[zp * 2, kc, pl.ds(CH // 2, CH // 2)]
         send(under, under, s_w, r_fp.at[kc], dev_zm)
-        if kc == 0:
-            send(wbuf.at[zm * 2, 0], wbuf.at[zm * 2 + 1, 0], s_w, r_pm, dev_ya)
-            send(wbuf.at[zp * 2, 0], wbuf.at[zp * 2 + 1, 0], s_w, r_pp, dev_ya)
 
     def late_own(kc):
         @pl.when(xh == 1)
@@ -317,8 +317,20 @@
         block = wbuf.at[z * 2 + 1, kc]
         wait_for(block, r_p.at[kc])
         if kc > 0:
-            send(block, block, s_w, r_pm, dev_zp)
-            send(block, block, s_w, r_pp, dev_zm)
+            send(block, block, s_p, r_pm, dev_zp)
+            send(block, block, s_p, r_pp, dev_zm)
+        else:
+            @pl.when(lax.div(z, 2) == xh)
+            def _():
+                send(block, block, s_p0, r_pm, dev_zp)
+                send(block, block, s_p0, r_pp, dev_zm)
+
+    def pair_first():
+        for near, sem in ((zm, r_pm), (zp, r_pp)):
+
+            @pl.when(lax.div(near, 2) != xh)
+            def _():
+                send(wbuf.at[near * 2, 0], wbuf.at[near * 2 + 1, 0], s_e, sem, dev_ya)
 
     def rows_x(n):
         wait_for(hid.at[1, n], r_h1.at[n])
@@ -473,12 +485,12 @@
         with jax.named_scope(label):
             work(*args)
 
+    step("far0", far, 0)
     step("rows_y0", rows_y, 0)
     late_own(3)
+    step("far1", far, 1)
     step("rows_y1", rows_y, 1)
     late_own(4)
-    step("far0", far, 0)
-    step("far1", far, 1)
     with jax.named_scope("text_in"):
         wait_for(text, lsem.at[NCH + 1])
     loop("text_step", 2, text_step)
@@ -486,30 +498,29 @@
     step("far2", far, 2)
     step("rows_y2", rows_y, 2)
     step("rows_x0", rows_x, 0)
+    step("across_y0", across_y, 0)
     step("far3", far, 3)
     step("rows_y3", rows_y, 3)
-    step("far4", far, 4)
-    step("pair01", pair, 0)
-    pair(1)
+    step("across_y1", across_y, 1)
     step("rows_x1", rows_x, 1)
     step("rows_y4", rows_y, 4)
-    pair(2)
-    pair(3)
-    pair(4)
+    step("far4", far, 4)
+    for kc in range(NCH):
+        step(f"pair{kc}", pair, kc)
     give_near(0)
-    step("across_y0", across_y, 0)
     step("rows_x2", rows_x, 2)
+    step("across_y2", across_y, 2)
+    take_near(0)
     give_near(2)
-    step("across_y1", across_y, 1)
-    take_near(0)
+    step("across_y3", across_y, 3)
     step("rows_x3", rows_x, 3)
-    step("across_y2", across_y, 2)
     take_near(2)
-    step("across_y3", across_y, 3)
+    step("across_y4", across_y, 4)
+    pair_first()
+    run_single("middle", middle, 0, [0])
     step("rows_x4", rows_x, 4)
     give_near(1)
-    step("across_y4", across_y, 4)
-    run_single("middle", middle, 0, [0, 1, 2])
+    run_single("middle", middle, 0, [1, 2])
     take_near(1)
     with jax.named_scope("diagonal"):
         wait_for(hid.at[3], r_h3)
@@ -562,7 +573,6 @@
     def _():
         finish(0, 1)
 
-    on_side(1, (finish, 0, (1, 3, 0, 2)))
     every = [0, 1, 2, 3]
     with jax.named_scope("pair_blocks_o"):
         wait_for(wbuf.at[zo * 2 + 1], r_p2)
@@ -572,14 +582,15 @@
     def _():
         finish(0, 1)
 
-    on_side(0, (onward, 0, (1,)), (finish, 0, (3,)), (onward, 0, (3,)))
-    on_side(1, (onward, 0, (1, 3, 0, 2)))
+    on_side(0, (onward, 0, (1,)))
+    on_side(1, (finish, 0, (1, 3, 0, 2)), (onward, 0, (1, 3, 0, 2)))
     with jax.named_scope("pair_blocks"):
         wait_for(wbuf.at[zm * 2 + 1], r_pm)
         wait_for(wbuf.at[zp * 2 + 1], r_pp)
     run_single("far_b", far_b, 1, every)
+    on_side(0, (finish, 0, (3,)), (onward, 0, (3,)))
+    run_single("far_c", far_c, 1, every)
     on_side(0, (finish, 0, (0,)), (onward, 0, (0,)))
-    run_single("far_c", far_c, 1, every)
     on_side(0, (finish, 0, (2,)), (onward, 0, (2,)))
     for r in (1, 0, 3, 2):
         finish(1, r)
@@ -605,7 +616,13 @@
     sums_copy = pltpu.make_async_copy(ibuf, isums_out, lsem.at[1])
     sums_copy.start()
 
-    wait_for(wbuf.at[pl.ds(0, 7)], s_w)
+    wait_for(wbuf.at[pl.ds(0, 5)], s_w)
+    wait_for(wbuf.at[pl.ds(0, 2), pl.ds(0, 4)], s_p)
+    wait_for(wbuf.at[0, 0], s_e)
+
+    @pl.when(lax.div(z, 2) == xh)
+    def _():
+        wait_for(wbuf.at[pl.ds(0, 2), 0], s_p0)
 
     @pl.when(xh == 1)
     def _():
@@ -813,6 +830,9 @@
             dma,
             dma,
             dma,
+            dma,
+            dma,
+            dma,
             dma((32,)),
             dma((3,)),
             dma((3,)),

time: 82 us -> 80.2 us (0.978)
  Pallas kernels: 80.9 us -> 79.2 us
    pallas_call x1, Pallas kernels: 76.6 us -> 74.8 us  [per_device(): pl.pallas_call(merge_kernel, out_shape=(jax.ShapeDtypeStruct((8, CH, CH),...]
where the time goes in v4:
time: 80.2 us; the launch traced here: 80 us
  Pallas kernels  79.2 us (99%)
    pallas_call x1, Pallas kernels, per_device(): pl.pallas_call(merge_kernel, out_shape=(jax.ShapeDtypeStruct((8, CH, CH),...  74.8 us
    pallas_call x1, Pallas kernels, per_device(): pl.pallas_call(splice_kernel, out_shape=(jax.ShapeDtypeStruct((seq, featu...  4.32 us

profile of v4, /device:TPU:1, one launch (start us, length us, event | category | flops | bytes accessed | tf_op | source)
XLA Modules:
  0.0 80.0 jit_solution(6326442154049087822)
XLA Ops:
  0.6 74.8 %merge.1 = (bf16[8,256,256]{2,1,0:T(8,128)(2,1)}, f32[4,8,512]{2,1,0:T(8,128)}, f32[4,8,256]{2,1,0:T(8,128)}) custom-call(s32[4,32]{1,0:T(4,128)} %bitcast.8, bf16[1024,1280]{1,0:T(8,128)(2,1)} %pat_hbm.1, f32[1280]{0:T(1024)} %gain_hbm.1, f32[1280]{0:T(1024)} %nbias_hbm.1, bf16[5120,1280]{1,0:T(8,128)(2,1)} %w1_hbm.1, f32[1280]{0:T(1024)} %b1_hbm.1, ...), custom_call_target="tpu_custom_call" | custom-call | tf_op jit(solution)/shard_map/merge/pallas_call | solution.py:791
  75.5 4.3 %splice.1 = (bf16[512,2048]{1,0:T(8,128)(2,1)}, bf16[512,2048]{1,0:T(8,128)(2,1)}) custom-call(s32[4,2,32]{2,1,0:T(2,128)} %bitcast.10, s32[4,32]{1,0:T(4,128)} %bitcast.9, bf16[512,2048]{1,0:T(8,128)(2,1)} %text_hbm.3, bf16[8,256,256]{2,1,0:T(8,128)(2,1)} %get-tuple-element.5.img_hbm, f32[4,8,512]{2,1,0:T(8,128)} %get-tuple-element.6.tsums_hbm, ...), custom_call_target="tpu_custom_call" | custom-call | tf_op jit(solution)/shard_map/splice/pallas_call | solution.py:871

commit v5 on v4

--- a/solution.py
+++ b/solution.py
@@ -468,14 +468,15 @@
         for j in range(8):
             values = text[rows, j * CH : (j + 1) * CH].astype(F32)
             total = total + values * values
-        tbuf[t, :, rows] = row_squares(total)
+        tbuf[:, rows] = row_squares(total)
         return carry
 
-    def share(buf, send_sems, recv_sems):
+    def share(buf, result, own_sem, send_sems, recv_sems):
+        pltpu.make_async_copy(buf, result.at[t], own_sem).start()
         for i in range(1, 4):
             send(
-                buf.at[t],
-                buf.at[t],
+                buf,
+                result.at[t],
                 send_sems.at[i - 1],
                 recv_sems.at[i - 1],
                 (d, lax.rem(t + i, 4)),
@@ -484,6 +485,47 @@
     def step(label, work, *args):
         with jax.named_scope(label):
             work(*args)
+
+    def target(r, k):
+        row_y = y + lax.div(r, 2) * (yb - y)
+        row_x = xl + lax.rem(r, 2) * (1 - 2 * xl)
+        return lax.rem(z * 8 + row_y * 2 + row_x + k, SHARDS)
+
+    def pieces(p, r, k):
+        rows = pl.ds(k * CAP, CAP)
+        return obuf.at[p, r, rows], img.at[column_of(p), rows]
+
+    def finish(p, r):
+        with jax.named_scope(f"finish{p}{r}"):
+            wait_for(xrecv.at[p, r], r_x.at[p * 4 + r])
+            obuf[p, r] = (fbuf[p, r] + xrecv[p, r].astype(F32)).astype(BF16)
+            for k in range(4):
+                e = target(r, k)
+                src, dst = pieces(p, r, k)
+
+                @pl.when(e == d)
+                def _():
+                    pltpu.make_async_copy(src, dst, r_i).start()
+
+                @pl.when((e != d) & (lax.div(e, 4) == lax.div(d, 4)))
+                def _():
+                    send(src, dst, s_i.at[p * 16 + r * 4 + k], r_i, (e, t))
+
+    def onward(p, r):
+        for k in range(1, 4):
+            e = target(r, k)
+            src, dst = pieces(p, r, k)
+
+            @pl.when(lax.div(e, 4) != lax.div(d, 4))
+            def _():
+                send(src, dst, s_i.at[p * 16 + r * 4 + k], r_i, (e, t))
+
+    def on_side(side, *work):
+        @pl.when(xh == side)
+        def _():
+            for do, p, rows in work:
+                for r in rows:
+                    do(p, r)
 
     step("far0", far, 0)
     step("rows_y0", rows_y, 0)
@@ -494,7 +536,7 @@
     with jax.named_scope("text_in"):
         wait_for(text, lsem.at[NCH + 1])
     loop("text_step", 2, text_step)
-    share(tbuf, s_t, r_t)
+    share(tbuf, tsums_out, lsem.at[2], s_t, r_t)
     step("far2", far, 2)
     step("rows_y2", rows_y, 2)
     step("rows_x0", rows_x, 0)
@@ -524,50 +566,10 @@
     take_near(1)
     with jax.named_scope("diagonal"):
         wait_for(hid.at[3], r_h3)
+    on_side(1, (finish, 0, (1, 0)))
     give_near(3)
     run_single("middle3", middle, 0, [3])
     take_near(3)
-
-    def target(r, k):
-        row_y = y + lax.div(r, 2) * (yb - y)
-        row_x = xl + lax.rem(r, 2) * (1 - 2 * xl)
-        return lax.rem(z * 8 + row_y * 2 + row_x + k, SHARDS)
-
-    def pieces(p, r, k):
-        rows = pl.ds(k * CAP, CAP)
-        return obuf.at[p, r, rows], img.at[column_of(p), rows]
-
-    def finish(p, r):
-        with jax.named_scope(f"finish{p}{r}"):
-            wait_for(xrecv.at[p, r], r_x.at[p * 4 + r])
-            obuf[p, r] = (fbuf[p, r] + xrecv[p, r].astype(F32)).astype(BF16)
-            for k in range(4):
-                e = target(r, k)
-                src, dst = pieces(p, r, k)
-
-                @pl.when(e == d)
-                def _():
-                    pltpu.make_async_copy(src, dst, r_i).start()
-
-                @pl.when((e != d) & (lax.div(e, 4) == lax.div(d, 4)))
-                def _():
-                    send(src, dst, s_i.at[p * 16 + r * 4 + k], r_i, (e, t))
-
-    def onward(p, r):
-        for k in range(1, 4):
-            e = target(r, k)
-            src, dst = pieces(p, r, k)
-
-            @pl.when(lax.div(e, 4) != lax.div(d, 4))
-            def _():
-                send(src, dst, s_i.at[p * 16 + r * 4 + k], r_i, (e, t))
-
-    def on_side(side, *work):
-        @pl.when(xh == side)
-        def _():
-            for do, p, rows in work:
-                for r in rows:
-                    do(p, r)
 
     @pl.when((xh == 0) & (t != zo))
     def _():
@@ -583,7 +585,7 @@
         finish(0, 1)
 
     on_side(0, (onward, 0, (1,)))
-    on_side(1, (finish, 0, (1, 3, 0, 2)), (onward, 0, (1, 3, 0, 2)))
+    on_side(1, (onward, 0, (1, 0)), (finish, 0, (3, 2)), (onward, 0, (3, 2)))
     with jax.named_scope("pair_blocks"):
         wait_for(wbuf.at[zm * 2 + 1], r_pm)
         wait_for(wbuf.at[zp * 2 + 1], r_pp)
@@ -604,17 +606,15 @@
     for b in range(8):
         values = img[b].astype(F32)
         total = total + values * values
-    ibuf[t] = row_squares(total)
-    share(ibuf, s_s, r_s)
+    ibuf[...] = row_squares(total)
+    share(ibuf, isums_out, lsem.at[1], s_s, r_s)
     for i in range(1, 4):
-        wait_for(tbuf.at[lax.rem(t + 4 - i, 4)], r_t.at[i - 1])
-    text_copy = pltpu.make_async_copy(tbuf, tsums_out, lsem.at[2])
-    text_copy.start()
+        wait_for(tsums_out.at[lax.rem(t + 4 - i, 4)], r_t.at[i - 1])
+    wait_for(tbuf, lsem.at[2])
     with jax.named_scope("sums_in"):
         for i in range(1, 4):
-            wait_for(ibuf.at[lax.rem(t + 4 - i, 4)], r_s.at[i - 1])
-    sums_copy = pltpu.make_async_copy(ibuf, isums_out, lsem.at[1])
-    sums_copy.start()
+            wait_for(isums_out.at[lax.rem(t + 4 - i, 4)], r_s.at[i - 1])
+    wait_for(ibuf, lsem.at[1])
 
     wait_for(wbuf.at[pl.ds(0, 5)], s_w)
     wait_for(wbuf.at[pl.ds(0, 2), pl.ds(0, 4)], s_p)
@@ -645,16 +645,14 @@
 
         loop("drain", 4, drain)
     for i in range(1, 4):
-        wait_for(tbuf.at[t], s_t.at[i - 1])
-        wait_for(ibuf.at[t], s_s.at[i - 1])
+        wait_for(tbuf, s_t.at[i - 1])
+        wait_for(ibuf, s_s.at[i - 1])
     img_copy.wait()
-    text_copy.wait()
-    sums_copy.wait()
 
 
 def splice_kernel(
-    grids_ref,
-    routing_ref,
+    grids_hbm,
+    routing_hbm,
     text_hbm,
     img_hbm,
     tsums_hbm,
@@ -662,6 +660,8 @@
     gain_hbm,
     emb_hbm,
     out_hbm,
+    grids_ref,
+    routing_ref,
     text,
     img,
     tsums,
@@ -698,10 +698,18 @@
         loads[i].start()
     whole.start()
     small[1].start()
+    tables = [
+        pltpu.make_async_copy(grids_hbm, grids_ref, in_sem.at[steps + 4]),
+        pltpu.make_async_copy(routing_hbm, routing_ref, in_sem.at[steps + 5]),
+    ]
+    for copy in tables:
+        copy.start()
     for i in order[steps - first :]:
         loads[i].start()
 
     d = lax.axis_index("dp")
+    for copy in tables:
+        copy.wait()
     starts = []
     total = jnp.int32(0)
     for k in range(4):
@@ -786,7 +794,6 @@
     seq, features = text_embeds.shape
     width = patches.shape[1]
     anywhere = pl.BlockSpec(memory_space=pl.ANY)
-    smem = pl.BlockSpec(memory_space=pltpu.SMEM)
     dma = pltpu.SemaphoreType.DMA
     img, tsums, isums = pl.pallas_call(
         merge_kernel,
@@ -818,8 +825,8 @@
             pltpu.VMEM((2, 4, CH, CH), F32),
             pltpu.VMEM((2, 4, CH, CH), BF16),
             pltpu.VMEM((8, CH, CH), BF16),
-            pltpu.VMEM((4, 8, seq), F32),
-            pltpu.VMEM((4, 8, CH), F32),
+            pltpu.VMEM((8, seq), F32),
+            pltpu.VMEM((8, CH), F32),
             dma((NCH + 2,)),
             dma((5,)),
             dma((NCH,)),
@@ -874,9 +881,11 @@
             jax.ShapeDtypeStruct((seq, features), BF16),
             jax.ShapeDtypeStruct((seq, features), BF16),
         ),
-        in_specs=[smem, smem] + [anywhere] * 5,
+        in_specs=[anywhere] * 7,
         out_specs=(anywhere, anywhere),
         scratch_shapes=[
+            pltpu.SMEM((image_grids.shape[1], 2, SHARDS), jnp.int32),
+            pltpu.SMEM(routing.T.shape, jnp.int32),
             pltpu.VMEM((seq, features), BF16),
             pltpu.VMEM(img.shape, BF16),
             pltpu.VMEM(tsums.shape, F32),
@@ -884,7 +893,7 @@
             pltpu.VMEM((1, features), F32),
             pltpu.VMEM((4 * CAP, features), BF16),
             pltpu.VMEM((seq, features), BF16),
-            dma((8,)),
+            dma((10,)),
             dma((4,)),
             dma((4,)),
         ],

time: 80.2 us -> 78.3 us (0.976)
  Pallas kernels: 79.2 us -> 77.4 us
    pallas_call x1, Pallas kernels: 74.8 us -> 73.8 us  [per_device(): pl.pallas_call(merge_kernel, out_shape=(jax.ShapeDtypeStruct((8, CH, CH),...]
where the time goes in v5:
time: 78.3 us; the launch traced here: 78.2 us
  Pallas kernels  77.4 us (99%)
  between operations  0.8 us (1%)
    pallas_call x1, Pallas kernels, per_device(): pl.pallas_call(merge_kernel, out_shape=(jax.ShapeDtypeStruct((8, CH, CH),...  73.8 us
    pallas_call x1, Pallas kernels, per_device(): pl.pallas_call(splice_kernel, out_shape=(jax.ShapeDtypeStruct((seq, featu...  3.59 us

profile of v5, /device:TPU:1, one launch (start us, length us, event | category | flops | bytes accessed | tf_op | source)
XLA Modules:
  0.0 78.2 jit_solution(3776186437345757219)
XLA Ops:
  0.6 73.8 %merge.1 = (bf16[8,256,256]{2,1,0:T(8,128)(2,1)}, f32[4,8,512]{2,1,0:T(8,128)}, f32[4,8,256]{2,1,0:T(8,128)}) custom-call(s32[4,32]{1,0:T(4,128)} %bitcast.8, bf16[1024,1280]{1,0:T(8,128)(2,1)} %pat_hbm.1, f32[1280]{0:T(1024)} %gain_hbm.1, f32[1280]{0:T(1024)} %nbias_hbm.1, bf16[5120,1280]{1,0:T(8,128)(2,1)} %w1_hbm.1, f32[1280]{0:T(1024)} %b1_hbm.1, ...), custom_call_target="tpu_custom_call" | custom-call | tf_op jit(solution)/shard_map/merge/pallas_call | solution.py:798
  74.4 3.6 %splice.1 = (bf16[512,2048]{1,0:T(8,128)(2,1)}, bf16[512,2048]{1,0:T(8,128)(2,1)}) custom-call(s32[4,2,32]{2,1,0:T(2,128)} %bitcast.10, s32[4,32]{1,0:T(4,128)} %bitcast.9, bf16[512,2048]{1,0:T(8,128)(2,1)} %text_hbm.3, bf16[8,256,256]{2,1,0:T(8,128)(2,1)} %get-tuple-element.5.img_hbm, f32[4,8,512]{2,1,0:T(8,128)} %get-tuple-element.6.tsums_hbm, ...), custom_call_target="tpu_custom_call" | custom-call | tf_op jit(solution)/shard_map/splice/pallas_call | solution.py:878

commit v6 on v5

--- a/solution.py
+++ b/solution.py
@@ -15,7 +15,7 @@
 D = 8192
 CH = 256
 NCH = 5
-HEADS = (128, 208)
+HEADS = (128, 192)
 SQRT_HALF = 0.7071067811865476
 
 
@@ -40,6 +40,7 @@
 
 
 def row_squares(values):
+    values = values[:, :128] + values[:, 128:]
     ones = jnp.ones((8, values.shape[1]), F32)
     return lax.dot_general(
         ones,
@@ -575,6 +576,7 @@
     def _():
         finish(0, 1)
 
+    on_side(1, (finish, 0, (3, 2)))
     every = [0, 1, 2, 3]
     with jax.named_scope("pair_blocks_o"):
         wait_for(wbuf.at[zo * 2 + 1], r_p2)
@@ -585,7 +587,7 @@
         finish(0, 1)
 
     on_side(0, (onward, 0, (1,)))
-    on_side(1, (onward, 0, (1, 0)), (finish, 0, (3, 2)), (onward, 0, (3, 2)))
+    on_side(1, (onward, 0, (1, 0, 3, 2)))
     with jax.named_scope("pair_blocks"):
         wait_for(wbuf.at[zm * 2 + 1], r_pm)
         wait_for(wbuf.at[zp * 2 + 1], r_pp)

time: 78.3 us -> 78.3 us (level)
  no operation moved by 1% of the time
where the time goes in v6:
time: 78.3 us; the launch traced here: 78.1 us
  Pallas kernels  77.3 us (99%)
  between operations  0.8 us (1%)
    pallas_call x1, Pallas kernels, per_device(): pl.pallas_call(merge_kernel, out_shape=(jax.ShapeDtypeStruct((8, CH, CH),...  73.7 us
    pallas_call x1, Pallas kernels, per_device(): pl.pallas_call(splice_kernel, out_shape=(jax.ShapeDtypeStruct((seq, featu...  3.58 us

profile of v6, /device:TPU:1, one launch (start us, length us, event | category | flops | bytes accessed | tf_op | source)
XLA Modules:
  0.0 78.1 jit_solution(1959075143614394424)
XLA Ops:
  0.6 73.7 %merge.1 = (bf16[8,256,256]{2,1,0:T(8,128)(2,1)}, f32[4,8,512]{2,1,0:T(8,128)}, f32[4,8,256]{2,1,0:T(8,128)}) custom-call(s32[4,32]{1,0:T(4,128)} %bitcast.8, bf16[1024,1280]{1,0:T(8,128)(2,1)} %pat_hbm.1, f32[1280]{0:T(1024)} %gain_hbm.1, f32[1280]{0:T(1024)} %nbias_hbm.1, bf16[5120,1280]{1,0:T(8,128)(2,1)} %w1_hbm.1, f32[1280]{0:T(1024)} %b1_hbm.1, ...), custom_call_target="tpu_custom_call" | custom-call | tf_op jit(solution)/shard_map/merge/pallas_call | solution.py:800
  74.4 3.6 %splice.1 = (bf16[512,2048]{1,0:T(8,128)(2,1)}, bf16[512,2048]{1,0:T(8,128)(2,1)}) custom-call(s32[4,2,32]{2,1,0:T(2,128)} %bitcast.10, s32[4,32]{1,0:T(4,128)} %bitcast.9, bf16[512,2048]{1,0:T(8,128)(2,1)} %text_hbm.3, bf16[8,256,256]{2,1,0:T(8,128)(2,1)} %get-tuple-element.5.img_hbm, f32[4,8,512]{2,1,0:T(8,128)} %get-tuple-element.6.tsums_hbm, ...), custom_call_target="tpu_custom_call" | custom-call | tf_op jit(solution)/shard_map/splice/pallas_call | solution.py:880
